TPU v7x, 256 devices: a whole 4x4x8 slice. The times are simulated.
256 devices in a mesh: chan: 4 (over z_lo, core), bl: 64 (over x, y, z_hi).
Axes of the slice: x: 4, y: 4, z: 8 (z_hi: 4, z_lo: 2; z = z_hi * 2 + z_lo), core: 2. Of those that a mesh axis runs over, the one named last changes fastest.
Arguments:
- vis_value: bfloat16 [4, 64, 2, 2048], P('chan', 'bl'), may hold values from -6 to 6
- vis_weight: bfloat16 [4, 64, 2048], P('chan', 'bl'), may hold values from 0.19921875 to 5
- kernel: bfloat16 [4, 64, 64, 2048], P('chan', 'bl'), may hold values from 0.049804688 to 1
- tile_index: int32 [4, 64, 2048], P('chan', 'bl'), may hold values from 0 to 262143
- plane_index: int32 [4, 64, 2048], P('chan', 'bl'), may hold values from 0 to 7
- chan_index: int32 [4, 64, 2048], P('chan', 'bl'), may hold values from 0 to 15
- chan_offset: float32 [4, 16], P('chan'), may hold values from -0.4 to 0.4
- counts: int32 [4, 64], P('chan', 'bl'), may hold values from 256 to 2048, as said below
Outputs:
- taylor_coeffs: float32 [3, 32768], P(None, ('chan', 'bl'))
Inputs may be any that keep to these rules, and one draw needn't show every extreme that they name: `counts`: each device's number of live visibility slots; slots from that number on are ignored. In every draw some device has exactly 2048.
All inputs are finite; a program needn't handle non-finite values.
Results may differ from a plain program's by a relative error of at most 0.0003.
Values may be sent and summed in bfloat16 or wider, within the bound.
A program may use at most 128 MiB of HBM per device.

v0:
```python
import functools

import jax
import jax.numpy as jnp
from jax import lax
from jax.sharding import Mesh
from jax.sharding import PartitionSpec as P

NPIX = 4096
TILE = 8
TAYLOR = 3
MOMENTS = 5
WPLANES = 8
STRIP = 8
BLK = 256
CHAN_BL = ("chan_0", "chan_1", "bl_0", "bl_1", "bl_2")
CHAN = ("chan_0", "chan_1")
BL = ("bl_0", "bl_1", "bl_2")


two_pi = 6.283185307179586
w_step = 40.0
inner_radix = 128
highest = lax.Precision.HIGHEST


def by_axis(array, axes):
    return functools.reduce(lax.psum, axes, array)


def split_up(array, dim, length):
    lengths = array.shape
    pieces = array.reshape(*lengths[:dim], length, lengths[dim] // length, *lengths[dim + 1 :])
    return jnp.moveaxis(pieces, dim, 0)


def sum_at_owner(array, axis, dim):
    pieces = split_up(array, dim, lax.axis_size(axis))
    arrived = lax.all_to_all(pieces, axis, split_axis=0, concat_axis=0, tiled=True)
    return arrived.sum(axis=0)


def block_terms(values, weights, kernel, tiles, planes, chans, offsets, live_mask):
    block_size = weights.shape[0]
    ntiles = NPIX // TILE
    channel_ids = jnp.arange(offsets.shape[0], dtype=jnp.int32)
    taylor_coord = jnp.sum(
        jnp.where(chans[:, None] == channel_ids[None, :], offsets[None, :], 0.0), axis=1
    )
    live_weight = jnp.where(live_mask, weights.astype(jnp.float32), 0.0)
    kernel_taps = kernel.astype(jnp.float32).reshape(TILE, TILE, block_size)
    strip_rows = jnp.arange(STRIP, dtype=jnp.int32) - STRIP // 2
    grid_cols = (
        (tiles // ntiles)[None, :] * TILE + jnp.arange(TILE, dtype=jnp.int32)[:, None] - NPIX // 2
    )
    phase_index = grid_cols[:, None, :] * strip_rows[None, :, None] % NPIX
    phase_angle = phase_index.astype(jnp.float32) * (two_pi / NPIX)
    cosine = jnp.cos(phase_angle)
    sine = jnp.sin(phase_angle)
    tile_real = jnp.sum(kernel_taps[:, :, None, :] * cosine[:, None, :, :], axis=0)
    tile_imag = jnp.sum(kernel_taps[:, :, None, :] * sine[:, None, :, :], axis=0)
    base_real = live_weight * values[0].astype(jnp.float32)
    base_imag = live_weight * values[1].astype(jnp.float32)
    power_list = [jnp.ones_like(taylor_coord)]
    for power_id in range(MOMENTS - 1):
        power_list.append(power_list[power_id] * taylor_coord)
    power_stack = jnp.stack(power_list[:TAYLOR], axis=0)
    coeff_real = (base_real[None, :] * power_stack)[None, :, None, :]
    coeff_imag = (base_imag[None, :] * power_stack)[None, :, None, :]
    part_real = coeff_real * tile_real[:, None] - coeff_imag * tile_imag[:, None]
    part_imag = coeff_real * tile_imag[:, None] + coeff_imag * tile_real[:, None]
    columns = TILE * TAYLOR * STRIP
    updates = jnp.stack(
        [part_real.reshape(columns, block_size), part_imag.reshape(columns, block_size)]
    )
    updates = jnp.transpose(updates, (0, 2, 1))
    target_rows = planes * ntiles + tiles % ntiles
    tap_sums = jnp.sum(kernel_taps, axis=(0, 1))
    weighted_taps = live_weight * tap_sums
    moment_add = jnp.stack(
        [jnp.sum(weighted_taps * power_list[moment_id]) for moment_id in range(MOMENTS)]
    )
    return (updates, target_rows, moment_add)


def grid_slots(arrays, low_limit, high_limit, offsets):
    slot_count = arrays[1].shape[0]
    middle = slot_count // 2
    ntiles = NPIX // TILE
    low_blocks = (jnp.minimum(low_limit, middle) + BLK - 1) // BLK
    high_blocks = (jnp.maximum(high_limit - middle, 0) + BLK - 1) // BLK

    def one_block(block_turn, state_pair):
        uv_grid, moments = state_pair
        block_id = jnp.where(
            block_turn < low_blocks, block_turn, middle // BLK + block_turn - low_blocks
        )
        first_slot = block_id * BLK
        slot_limit = jnp.where(first_slot < middle, low_limit, high_limit)
        live_mask = first_slot + jnp.arange(BLK, dtype=jnp.int32) < slot_limit
        pieces = [
            lax.dynamic_slice_in_dim(source, first_slot, BLK, source.ndim - 1) for source in arrays
        ]
        updates, target_rows, moment_add = block_terms(
            pieces[0], pieces[1], pieces[2], pieces[3], pieces[4], pieces[5], offsets, live_mask
        )
        return (uv_grid.at[:, target_rows].add(updates), moments + moment_add)

    initial = (
        jnp.zeros((2, WPLANES * ntiles, TILE * TAYLOR * STRIP), jnp.float32),
        jnp.zeros((MOMENTS,), jnp.float32),
    )
    return lax.fori_loop(0, low_blocks + high_blocks, one_block, initial)


def complex_table(cosine, sine):
    return jnp.stack(
        [jnp.stack([cosine, -sine], axis=0), jnp.stack([sine, cosine], axis=0)], axis=0
    )


def screen_grid(plane_ids, column_grid):
    cell_size = 0.5 / NPIX
    strip_rows = jnp.arange(STRIP, dtype=jnp.int32) - STRIP // 2
    xcoord = strip_rows.astype(jnp.float32) * cell_size
    ycoord = (column_grid - NPIX // 2).astype(jnp.float32) * cell_size
    radius = xcoord[:, None, None] * xcoord[:, None, None] + ycoord[None] * ycoord[None]
    lowered = -radius / (1.0 + jnp.sqrt(1.0 - radius))
    w_value = w_step * (plane_ids.astype(jnp.float32) - 0.5 * (WPLANES - 1))
    return two_pi * w_value[:, None, None, None] * lowered[None]


def strip_image(uv_grid):
    ntiles = NPIX // TILE
    outer = NPIX // inner_radix
    sub_tiles = inner_radix // TILE
    width = TAYLOR * STRIP
    plane_count = uv_grid.shape[1] // ntiles
    cube = uv_grid.reshape(2, plane_count, outer, sub_tiles, TILE, width)
    cube = jnp.transpose(cube, (0, 1, 5, 2, 3, 4)).reshape(
        2, plane_count, width, outer, inner_radix
    )
    outer_ids = jnp.arange(outer, dtype=jnp.int32)
    inner_ids = jnp.arange(inner_radix, dtype=jnp.int32)
    angle_outer = (outer_ids[:, None] * outer_ids[None, :] % outer).astype(jnp.float32) * (
        two_pi / outer
    )
    table_outer = complex_table(jnp.cos(angle_outer), jnp.sin(angle_outer))
    section_one = jnp.einsum("oiav,ipRvn->opRan", table_outer, cube, precision=highest)
    twist_angle = (outer_ids[:, None] * inner_ids[None, :] % NPIX).astype(jnp.float32) * (
        two_pi / NPIX
    )
    twist_sign = 1.0 - 2.0 * (inner_ids % 2).astype(jnp.float32)
    twist_real = jnp.cos(twist_angle) * twist_sign
    twist_imag = jnp.sin(twist_angle) * twist_sign
    twisted = jnp.stack(
        [
            section_one[0] * twist_real - section_one[1] * twist_imag,
            section_one[0] * twist_imag + section_one[1] * twist_real,
        ]
    )
    angle_inner = (inner_ids[:, None] * inner_ids[None, :] % inner_radix).astype(jnp.float32) * (
        two_pi / inner_radix
    )
    table_inner = complex_table(jnp.cos(angle_inner), jnp.sin(angle_inner))
    section_two = jnp.einsum("oicn,ipRan->opRac", table_inner, twisted, precision=highest)
    column_grid = inner_ids[None, :] * outer + outer_ids[:, None]
    parity = 1.0 - 2.0 * (column_grid % 2).astype(jnp.float32)
    angles = screen_grid(jnp.arange(plane_count, dtype=jnp.int32), column_grid)
    spectra = section_two.reshape(2, plane_count, TAYLOR, STRIP, outer, inner_radix)
    image = jnp.sum(
        parity * (jnp.cos(angles)[:, None] * spectra[0] - jnp.sin(angles)[:, None] * spectra[1]),
        axis=0,
    )
    return jnp.transpose(image, (0, 1, 3, 2)).reshape(TAYLOR, STRIP * NPIX)


def solve_taylor(moments, images):
    entry_00, entry_01, entry_02 = (moments[0], moments[1], moments[2])
    entry_11, entry_12, entry_22 = (moments[2], moments[3], moments[4])
    minor_00 = entry_11 * entry_22 - entry_12 * entry_12
    minor_01 = entry_02 * entry_12 - entry_01 * entry_22
    minor_02 = entry_01 * entry_12 - entry_02 * entry_11
    minor_11 = entry_00 * entry_22 - entry_02 * entry_02
    minor_12 = entry_01 * entry_02 - entry_00 * entry_12
    minor_22 = entry_00 * entry_11 - entry_01 * entry_01
    determinant = entry_00 * minor_00 + entry_01 * minor_01 + entry_02 * minor_02
    first = (minor_00 * images[0] + minor_01 * images[1] + minor_02 * images[2]) / determinant
    second = (minor_01 * images[0] + minor_11 * images[1] + minor_12 * images[2]) / determinant
    third = (minor_02 * images[0] + minor_12 * images[1] + minor_22 * images[2]) / determinant
    return jnp.stack([first, second, third])


def body(vis_value, vis_weight, kernel, tile_index, plane_index, chan_index, chan_offset, counts):
    own_arrays = (
        vis_value[0, 0],
        vis_weight[0, 0],
        kernel[0, 0],
        tile_index[0, 0],
        plane_index[0, 0],
        chan_index[0, 0],
    )
    own_count = counts[0, 0]
    offsets = chan_offset[0]
    uv_grid, moments = grid_slots(own_arrays, own_count, own_count, offsets)
    moments_total = by_axis(moments, CHAN_BL)
    image = strip_image(uv_grid)
    group_share = sum_at_owner(image, CHAN, 1)
    image_share = sum_at_owner(group_share, BL, 1)
    return solve_taylor(moments_total, image_share)


def solution(mesh):
    split = Mesh(mesh.devices.reshape(2, 2, 4, 4, 4), ("chan_0", "chan_1", "bl_0", "bl_1", "bl_2"))
    return jax.shard_map(
        body,
        mesh=split,
        in_specs=(
            P(CHAN, BL, None, None),
            P(CHAN, BL, None),
            P(CHAN, BL, None, None),
            P(CHAN, BL, None),
            P(CHAN, BL, None),
            P(CHAN, BL, None),
            P(CHAN, None),
            P(CHAN, BL),
        ),
        out_specs=P(None, CHAN_BL),
        check_vma=False,
    )
```

profile of v0, /device:TPU:32, one launch (start us, length us, event | category | flops | bytes accessed | tf_op | source)
XLA Modules:
  0.0 480.9 jit_solution(6700756206202135942)
XLA Ops:
  1.5 0.7 reduce.2
  2.2 5.4 %broadcast_in_dim.59 = f32[2,4096,192]{2,0,1:T(2,128)} broadcast(f32[]{:T(128)} %constant.237.clone.1), dimensions={} | broadcast | bytes 6291460 | tf_op jit(solution)/shard_map/broadcast_in_dim | solution.py:110
  7.6 106.6 %while.15 = (s32[]{:T(128)}, f32[2,4096,192]{2,0,1:T(2,128)}, f32[5]{0:T(128)S(1)}, s32[]{:T(128)}, s32[]{:T(128)}, /*index=5*/s32[2048]{0:T(1024)}, s32[2048]{0...) while((s32[]{:T(128)}, f32[2,4096,192]{2,0,1:T(2,128)}, ...), condition=%wide.region_11.12_spmd, body=%wide.region_0.11_spmd.sunk | while | flops 1292563 | bytes 3926113 | solution.py:113
  7.6 0.8 fusion.75
  8.8 0.8 convert_bitcast_fusion.2
  9.6 0.8 dynamic-slice_convert_fusion.3
  10.5 0.8 convert_reduce_fusion.2
  11.3 0.7 fusion.77
  12.0 0.8 dynamic_slice.69
  13.2 26.2 %scatter_fusion = f32[2,4096,192]{2,0,1:T(2,128)} fusion(f32[2,4096,192]{2,0,1:T(2,128)} %get-tuple-element.435, s32[256]{0:T(256)S(1)} %get-tuple-element.393, f32[256,2,192]{2,1,0:T(2,128)S(1)} %copy.37), kind=kCustom, calls=%fused_computation.clone.1 | custom fusion | flops 98304 | bytes 1180672 | tf_op jit(solution)/shard_map/while/body/scatter-add | solution.py:107
  39.4 0.7 fusion.79
  40.1 3.1 stack.120
  43.2 0.8 fusion.75
  44.4 0.8 convert_bitcast_fusion.2
  45.2 0.8 dynamic-slice_convert_fusion.3
  46.1 0.8 convert_reduce_fusion.2
  46.9 0.7 fusion.77
  47.6 0.8 dynamic_slice.69
  48.8 26.0 %scatter_fusion = f32[2,4096,192]{2,0,1:T(2,128)} fusion(f32[2,4096,192]{2,0,1:T(2,128)} %get-tuple-element.435, s32[256]{0:T(256)S(1)} %get-tuple-element.393, f32[256,2,192]{2,1,0:T(2,128)S(1)} %copy.37), kind=kCustom, calls=%fused_computation.clone.1 | custom fusion | flops 98304 | bytes 1180672 | tf_op jit(solution)/shard_map/while/body/scatter-add | solution.py:107
  74.9 0.7 fusion.79
  75.6 3.1 stack.120
  78.7 0.8 fusion.75
  79.8 0.8 convert_bitcast_fusion.2
  80.7 0.8 dynamic-slice_convert_fusion.3
  81.5 0.8 convert_reduce_fusion.2
  82.3 0.7 fusion.77
  83.0 0.8 dynamic_slice.69
  84.3 26.0 %scatter_fusion = f32[2,4096,192]{2,0,1:T(2,128)} fusion(f32[2,4096,192]{2,0,1:T(2,128)} %get-tuple-element.435, s32[256]{0:T(256)S(1)} %get-tuple-element.393, f32[256,2,192]{2,1,0:T(2,128)S(1)} %copy.37), kind=kCustom, calls=%fused_computation.clone.1 | custom fusion | flops 98304 | bytes 1180672 | tf_op jit(solution)/shard_map/while/body/scatter-add | solution.py:107
  110.3 0.7 fusion.79
  111.0 3.1 stack.120
  114.3 7.2 %copy.21 = f32[2,4096,192]{2,1,0:T(8,128)} copy(f32[2,4096,192]{2,0,1:T(2,128)} %get-tuple-element.222) | data formatting | bytes 12582912 | tf_op jit(solution)/shard_map/while | solution.py:113
  121.5 21.8 %reshape.607 = f32[2,8,32,16,8,24]{5,4,3,2,1,0:T(8,128)} reshape(f32[2,4096,192]{2,1,0:T(8,128)} %copy.21) | data formatting | bytes 12582912 | tf_op jit(solution)/shard_map/reshape | solution.py:139
  143.3 36.3 %copy.26 = f32[2,8,24,32,128,1]{3,4,0,5,2,1:T(8,128)} copy(f32[2,8,24,32,128,1]{2,4,3,1,0,5:T(8,128)} %bitcast.108) | data formatting | bytes 12582912 | tf_op jit(solution)/shard_map/reshape | solution.py:140
  179.9 3.7 multiply_cosine_fusion
  183.6 28.6 %convolution_bitcast_fusion = f32[2,8,24,32,128]{4,3,0,2,1:T(8,128)S(1)} fusion(f32[2,8,24,32,128,1]{3,4,0,5,2,1:T(8,128)} %copy.26, f32[1,2,32,32]{3,2,1,0:T(8,128)S(1)} %get-tuple-element.276, f32[1,2,32,32]{3,2,1,0:T(8,128)S(1)} %get-tuple-element.275), kind=kOutput, calls=%fused_computation.62 | convolution fusion | flops 1207963648 | bytes 12599296 | tf_op jit(solution)/shard_map/oiav,ipRvn->opRan/dot_general | solution.py:149
  212.2 0.9 multiply_subtract_fusion.1
  213.2 5.1 %fusion.24 = f32[2,8,24,32,128]{4,3,0,2,1:T(8,128)S(1)} fusion(f32[1,8,24,32,128]{4,3,0,2,1:T(8,128)S(1)} %get-tuple-element.270, f32[1,8,24,32,128]{4,3,0,2,1:T(8,128)S(1)} %get-tuple-element.269, f32[1,2,128,128]{3,2,1,0:T(8,128)S(1)} %get-tuple-element.274, f32[1,2,128,128]{3,2,1,0:T(8,128)S(1)} %get-tuple-element.273), kind=kOutput, calls=%fused_computation.61 | convolution fusion | flops 4833476608 | bytes 12845056 | tf_op jit(solution)/shard_map/oicn,ipRan->opRac/dot_general | solution.py:166
  219.1 1.6 fusion.23
  221.2 0.7 reshape_reshape.3
  222.2 117.6 %all_to_all.10 = f32[4,3,8192]{2,1,0:T(4,128)S(1)} all-to-all(f32[4,3,8192]{2,1,0:T(4,128)S(1)} %copy.25), channel_id=1, replica_groups=mesh['chan_0'=2,'chan_1'=2,'bl_0'=4,'bl_1'=4,'bl_2'=4] {'chan_0','chan_1'}, dimensions={0} | all-to-all | bytes 786432 | tf_op jit(solution)/shard_map/all_to_all | solution.py:39
  339.8 0.7 reduce_sum.148
  340.6 82.4 %all-to-all-start.1 = ((f32[64,3,128]{2,1,0:T(4,128)}), f32[64,3,128]{2,1,0:T(4,128)S(1)}, u32[]{:S(2)}, u32[]{:S(2)}) async-start(f32[64,3,128]{2,1,0:T(4,128)} %bitcast.49), calls=%async_computation.1 | async-start | bytes 262144 | tf_op jit(solution)/shard_map/all_to_all | solution.py:39
  422.9 5.0 %psum.35 = f32[5]{0:T(128)S(1)} all-reduce(f32[5]{0:T(128)S(1)} %get-tuple-element.221), channel_id=1, replica_groups=mesh['chan_0'=2,'chan_1'=2,'bl_0'=4,'bl_1'=4,'bl_2'=4] {'chan_0'}, use_global_device_ids=true, to_apply=%region_12.13 | all-reduce | flops 5 | bytes 40 | tf_op jit(solution)/shard_map/psum | solution.py:28
  427.9 2.4 psum.36
  430.4 10.7 %psum.37 = f32[5]{0:T(128)S(1)} all-reduce(f32[5]{0:T(128)S(1)} %psum.36), channel_id=1, replica_groups=mesh['chan_0'=2,'chan_1'=2,'bl_0'=4,'bl_1'=4,'bl_2'=4] {'bl_0'}, use_global_device_ids=true, to_apply=%region_14.15 | all-reduce | flops 5 | bytes 40 | tf_op jit(solution)/shard_map/psum | solution.py:28
  441.0 10.5 %psum.38 = f32[5]{0:T(128)S(1)} all-reduce(f32[5]{0:T(128)S(1)} %psum.37), channel_id=1, replica_groups=mesh['chan_0'=2,'chan_1'=2,'bl_0'=4,'bl_1'=4,'bl_2'=4] {'bl_1'}, use_global_device_ids=true, to_apply=%region_15.16 | all-reduce | flops 5 | bytes 40 | tf_op jit(solution)/shard_map/psum | solution.py:28
  451.5 12.2 %psum.39 = f32[5]{0:T(128)S(1)} all-reduce(f32[5]{0:T(128)S(1)} %psum.38), channel_id=1, replica_groups=mesh['chan_0'=2,'chan_1'=2,'bl_0'=4,'bl_1'=4,'bl_2'=4] {'bl_2'}, use_global_device_ids=true, to_apply=%region_16.17 | all-reduce | flops 5 | bytes 40 | tf_op jit(solution)/shard_map/psum | solution.py:28
  463.7 0.7 fusion.68
  (60 shorter events, 6.0 us)
Async XLA Ops:
  2.2 5.4 %copy-start = (f32[1,16]{1,0:T(1,128)S(1)}, f32[1,16]{1,0:T(1,128)}, u32[]{:S(2)}) copy-start(f32[1,16]{1,0:T(1,128)} %param.16) | copy-start | bytes 196
  340.6 139.6 %all-to-all-start.1 = ((f32[64,3,128]{2,1,0:T(4,128)}), f32[64,3,128]{2,1,0:T(4,128)S(1)}, u32[]{:S(2)}, u32[]{:S(2)}) async-start(f32[64,3,128]{2,1,0:T(4,128)} %bitcast.49), calls=%async_computation.1 | async-start | bytes 262144 | tf_op jit(solution)/shard_map/all_to_all | solution.py:39
where the time goes:
time: 489 us; the launch traced here: 481 us
  blocking collectives  158 us (32%)
  other arithmetic  103 us (21%)
  local copies, waits for them, and re-layouts  86 us (18%)
  starting transfers between devices  82.4 us (17%)
  matrix products  33.7 us (7%)
  between operations  16.7 us (3%)
    all_to_all x1, blocking collectives, sum_at_owner(): lax.all_to_all(pieces, axis, split_axis=0, concat_axis=0, tiled=True)  118 us
    all_to_all x1, starting transfers between devices, sum_at_owner(): lax.all_to_all(pieces, axis, split_axis=0, concat_axis=0, tiled=True)  82.4 us
    scatter-add x3, other arithmetic, one_block(): return (uv_grid.at[:, target_rows].add(updates), moments + moment_add)  78.3 us
    psum x5, blocking collectives, by_axis(): return functools.reduce(lax.psum, axes, array)  40.8 us
    reshape x1, local copies, waits for them, and re-layouts, strip_image(): jnp.transpose(cube, (0, 1, 5, 2, 3, 4))  36.3 us
    dot_general x1, matrix products, strip_image(): jnp.einsum('oiav,ipRvn->opRan', table_outer, cube, precision=highest)  28.6 us
    reshape x1, local copies, waits for them, and re-layouts, strip_image(): cube = uv_grid.reshape(2, plane_count, outer, sub_tiles, TILE, width)  21.8 us
  transfers between devices with their start and end apart: 1, of which 0 were waited for; matrix products, arithmetic and copies ran while one was open for 0% of the time, Pallas kernels for 0%

commit v1 on v0

v1 whole, which is shorter than its diff:
```python
import functools
import math

import jax
import jax.numpy as jnp
import numpy as np
from jax import lax
from jax.experimental import pallas as pl
from jax.experimental.pallas import tpu as pltpu
from jax.sharding import Mesh
from jax.sharding import PartitionSpec as P

NPIX = 4096
TILE = 8
TAYLOR = 3
MOMENTS = 5
STRIP = 8
SLOTS = 2048
HALF_PLANES = 4
WIDE = TILE + 1
ROWS = TAYLOR * WIDE * 2 * STRIP
CELLS = HALF_PLANES * NPIX // TILE
BLOCKS = 32
LANES = 128
CHUNK = 256
CHAN_BL = ("chan_0", "chan_1", "bl_0", "bl_1", "bl_2")
CHAN = ("chan_0", "chan_1")
BL = ("bl_0", "bl_1", "bl_2")
f32 = jnp.float32
bf16 = jnp.bfloat16


def split_pair(table):
    high = table.astype(np.float32).astype(bf16)
    low = (table - high.astype(np.float64)).astype(np.float32).astype(bf16)
    return high, low


def tap_table():
    a = np.arange(TILE)[None, :]
    l = np.arange(STRIP)[:, None] - STRIP // 2
    angle = 2.0 * math.pi * ((a - NPIX // 2) * l % NPIX) / NPIX
    table = np.zeros((2, TILE, STRIP, TILE, TILE))
    for e in range(TILE):
        table[0, e, :, :, e] = np.cos(angle)
        table[1, e, :, :, e] = np.sin(angle)
    high, low = split_pair(table.reshape(2 * TILE * STRIP, TILE * TILE))
    ones = np.zeros((16, TILE * TILE), np.float32)
    ones[0] = 1.0
    return np.concatenate([high, low, ones.astype(bf16)], axis=0)


def line_table():
    n = np.arange(LANES)
    angle = 2.0 * math.pi * (n[:, None] * n[None, :] % LANES) / LANES
    sign = 1.0 - 2.0 * (n % 2)
    c, s = np.cos(angle) * sign, np.sin(angle) * sign
    return np.concatenate(split_pair(np.block([[c, s], [-s, c]])), axis=0)


def twist_table():
    mq = np.arange(LANES)
    rows = [2.0 * math.pi * 8 * vb * mq / NPIX for vb in range(4)]
    for e in range(TILE):
        for mr in range(4):
            rows.append(2.0 * math.pi * e * (mq + LANES * mr) / NPIX + math.pi * e)
    angle = np.stack(rows)
    return np.concatenate([np.cos(angle), np.sin(angle)], axis=0).astype(np.float32)


def screen_table():
    cell = 0.5 / NPIX
    l = np.arange(STRIP)[None, :, None] - STRIP // 2
    m = (np.arange(BLOCKS)[:, None, None] - BLOCKS // 2) * LANES + np.arange(LANES)[None, None, :]
    radius = (l * cell) ** 2 + (m * cell) ** 2
    s = -radius / (1.0 + np.sqrt(1.0 - radius))
    angle = 2.0 * math.pi * 20.0 * s
    return np.stack([np.cos(angle), np.sin(angle)]).astype(np.float32)


def unit_circle(index):
    quarter = ((index + 64) >> 7) & 3
    x = (((index + 64) & 127) - 64).astype(f32) * (2.0 * math.pi / 512.0)
    x2 = x * x
    s = x * (1.0 + x2 * (-1.0 / 6 + x2 * (1.0 / 120 + x2 * (-1.0 / 5040 + x2 * (1.0 / 362880)))))
    c = 1.0 + x2 * (-0.5 + x2 * (1.0 / 24 + x2 * (-1.0 / 720 + x2 * (1.0 / 40320))))
    odd = (quarter & 1) == 1
    cos = jnp.where(odd, s, c)
    sin = jnp.where(odd, c, s)
    cos = jnp.where((quarter == 1) | (quarter == 2), -cos, cos)
    sin = jnp.where(quarter >= 2, -sin, sin)
    return cos, sin


def cmul(a, b):
    return a[0] * b[0] - a[1] * b[1], a[0] * b[1] + a[1] * b[0]


def cadd(a, b):
    return a[0] + b[0], a[1] + b[1]


def csub(a, b):
    return a[0] - b[0], a[1] - b[1]


def turn(a):
    return -a[1], a[0]


def four_point(x):
    a, b = cadd(x[0], x[2]), csub(x[0], x[2])
    c, d = cadd(x[1], x[3]), turn(csub(x[1], x[3]))
    return [cadd(a, c), cadd(b, d), csub(a, c), csub(b, d)]


def eight_point(x):
    even, odd = four_point(x[0::2]), four_point(x[1::2])
    r = math.sqrt(0.5)
    odd = [
        odd[0],
        ((odd[1][0] - odd[1][1]) * r, (odd[1][0] + odd[1][1]) * r),
        turn(odd[2]),
        ((-odd[3][0] - odd[3][1]) * r, (odd[3][0] - odd[3][1]) * r),
    ]
    return [cadd(e, o) for e, o in zip(even, odd)] + [csub(e, o) for e, o in zip(even, odd)]


def image_kernel(
    count_ref, offset_ref, vis_ref, weight_ref, kernel_ref, tile_ref, plane_ref, chan_ref,
    tap_ref, line_ref, twist_ref, screen_ref, out_ref, taps, updates, cell_of, grid, lines, screens, image,
):
    taps[...] = jnp.dot(tap_ref[...], kernel_ref[...], preferred_element_type=f32)
    count = count_ref[0, 0]

    def one_chunk(step, sums):
        at = pl.ds(pl.multiple_of(step * CHUNK, CHUNK), CHUNK)
        slot = step * CHUNK + lax.broadcasted_iota(jnp.int32, (1, CHUNK), 1)
        weight = jnp.where(slot < count, weight_ref[:, at].astype(f32), 0.0)
        chan = chan_ref[:, at]
        coord = jnp.zeros((1, CHUNK), f32)
        for c in range(16):
            coord = jnp.where(chan == c, offset_ref[0, c], coord)
        tile = tile_ref[:, at]
        plane = plane_ref[:, at]
        direct = plane >= HALF_PLANES
        tile_v = tile & 511
        tile_v = jnp.where(direct, tile_v, 511 - tile_v)
        half = jnp.where(direct, plane - HALF_PLANES, HALF_PLANES - 1 - plane)
        cell = half * 512 + (tile_v & 3) * LANES + (tile_v >> 2)
        cell_of[at, :] = jnp.transpose(jnp.broadcast_to(cell.astype(f32), (LANES, CHUNK)))
        weighted = weight * taps[256:257, at]
        new_sums = []
        power = weighted
        for m in range(MOMENTS):
            new_sums.append(sums[m] + power)
            power = power * coord
        vis = vis_ref[:, at].astype(f32)
        base = (weight * vis[0:1], weight * vis[1:2])
        row = lax.broadcasted_iota(jnp.int32, (STRIP, CHUNK), 0) - STRIP // 2
        phase = unit_circle(((tile >> 9) * row) & 511)
        turned = cmul(phase, base)
        mirror = jnp.where(direct, 1.0, -1.0)
        flipped = (turned[0] * mirror, turned[1] * mirror)
        direct_rows = jnp.broadcast_to(direct, (STRIP, CHUNK))
        coord_rows = jnp.broadcast_to(coord, (STRIP, CHUNK))
        parts = []
        for e in range(TILE):
            r = slice(e * STRIP, (e + 1) * STRIP)
            i = slice(64 + e * STRIP, 64 + (e + 1) * STRIP)
            tap_r = taps[r, at] + taps[128 + r.start:128 + r.stop, at]
            tap_i = taps[i, at] + taps[128 + i.start:128 + i.stop, at]
            parts.append(
                (turned[0] * tap_r - turned[1] * tap_i, flipped[0] * tap_i + flipped[1] * tap_r)
            )
        zero = jnp.zeros((STRIP, CHUNK), f32)
        for e in range(WIDE):
            there = parts[e] if e < TILE else (zero, zero)
            back = parts[TILE - e] if e > 0 else (zero, zero)
            both = jnp.concatenate(
                [jnp.where(direct_rows, there[0], back[0]), jnp.where(direct_rows, there[1], back[1])], axis=0
            )
            for k in range(TAYLOR):
                if k > 0:
                    both = both * jnp.concatenate([coord_rows, coord_rows], axis=0)
                high = both.astype(bf16)
                low = (both - high.astype(f32)).astype(bf16)
                first = (k * WIDE + e) * 16
                updates[first:first + 16, at] = high
                updates[ROWS + first:ROWS + first + 16, at] = low
        return tuple(new_sums)

    sums = lax.fori_loop(
        0, SLOTS // CHUNK, one_chunk, tuple(jnp.zeros((1, CHUNK), f32) for _ in range(MOMENTS))
    )
    lane = lax.broadcasted_iota(jnp.int32, (STRIP, LANES), 1)
    moment_row = jnp.zeros((STRIP, LANES), f32)
    for m in range(MOMENTS):
        total = jnp.sum(sums[m], axis=1, keepdims=True)
        moment_row = jnp.where(lane == m, jnp.broadcast_to(total, (STRIP, LANES)), moment_row)

    def one_stretch(step, carry):
        first = step * CHUNK
        cells = cell_of[...]
        pos = lax.broadcasted_iota(jnp.int32, (1, LANES), 1) + first
        hot = jnp.concatenate(
            [
                jnp.where(cells == (pos + half * LANES).astype(f32), 1.0, 0.0).astype(bf16)
                for half in range(CHUNK // LANES)
            ],
            axis=1,
        )
        both = jnp.dot(updates[...], hot, preferred_element_type=f32)
        grid[:, pl.ds(pl.multiple_of(first, CHUNK), CHUNK)] = both[:ROWS] + both[ROWS:]
        return carry

    lax.fori_loop(0, CELLS // CHUNK, one_stretch, 0)

    for b in range(BLOCKS):
        one = (screen_ref[0, b], screen_ref[1, b])
        two = cmul(one, one)
        for q in range(HALF_PLANES):
            screens[q, 0, b] = one[0]
            screens[q, 1, b] = one[1]
            if q < HALF_PLANES - 1:
                one = cmul(one, two)

    def piece(k, e, part, q, vb):
        first = ((k * WIDE + e) * 2 + part) * STRIP
        at = pl.ds(pl.multiple_of(q * 512 + vb * LANES, LANES), LANES)
        return grid[first:first + STRIP, at]

    def one_plane(q, carry):
        for k in range(TAYLOR):
            residues = []
            for vb in range(4):
                halves = []
                for part in range(2):
                    spill = piece(k, TILE, part, q, (vb - 1) % 4)
                    if vb == 0:
                        spill = pltpu.roll(spill, 1, 1)
                    column = [piece(k, 0, part, q, vb) + spill]
                    column += [piece(k, e, part, q, vb) for e in range(1, TILE)]
                    halves.append(jnp.concatenate(column, axis=0))
                residues.append(jnp.concatenate(halves, axis=1))
            whole = jnp.concatenate(residues, axis=0)
            high = whole.astype(bf16)
            low = (whole - high.astype(f32)).astype(bf16)
            lines[...] = (
                jnp.dot(high, line_ref[0:256], preferred_element_type=f32)
                + jnp.dot(low, line_ref[0:256], preferred_element_type=f32)
                + jnp.dot(high, line_ref[256:512], preferred_element_type=f32)
            )
            quarters = [[], [], [], []]
            for e in range(TILE):
                x = []
                for vb in range(4):
                    first = (vb * TILE + e) * STRIP
                    value = (lines[first:first + STRIP, 0:LANES], lines[first:first + STRIP, LANES:2 * LANES])
                    if vb > 0:
                        value = cmul(value, (twist_ref[vb:vb + 1], twist_ref[36 + vb:37 + vb]))
                    x.append(value)
                for mr, value in enumerate(four_point(x)):
                    if e > 0:
                        t = 4 + e * 4 + mr
                        value = cmul(value, (twist_ref[t:t + 1], twist_ref[36 + t:37 + t]))
                    quarters[mr].append(value)
            for mr in range(4):
                for mh, value in enumerate(eight_point(quarters[mr])):
                    b = 4 * mh + mr
                    add = value[0] * screens[q, 0, b] - value[1] * screens[q, 1, b]
                    image[k, b] = image[k, b] + add
        return carry

    image[...] = jnp.zeros_like(image)
    lax.fori_loop(0, HALF_PLANES, one_plane, 0)
    for b in range(BLOCKS):
        for k in range(TAYLOR):
            out_ref[pl.ds(b * 4 + k, STRIP, stride=LANES), :] = image[k, b]
        out_ref[pl.ds(b * 4 + TAYLOR, STRIP, stride=LANES), :] = moment_row


def device_image(counts, offsets, vis, weight, kernel, tile, plane, chan):
    smem = pl.BlockSpec(memory_space=pltpu.SMEM)
    vmem = pl.BlockSpec(memory_space=pltpu.VMEM)
    return pl.pallas_call(
        image_kernel,
        out_shape=jax.ShapeDtypeStruct((STRIP * BLOCKS * 4, LANES), f32),
        in_specs=[smem, smem] + [vmem] * 10,
        out_specs=vmem,
        scratch_shapes=[
            pltpu.VMEM((272, SLOTS), f32),
            pltpu.VMEM((2 * ROWS, SLOTS), bf16),
            pltpu.VMEM((SLOTS, LANES), f32),
            pltpu.VMEM((ROWS, CELLS), f32),
            pltpu.VMEM((256, 256), f32),
            pltpu.VMEM((HALF_PLANES, 2, BLOCKS, STRIP, LANES), f32),
            pltpu.VMEM((TAYLOR, BLOCKS, STRIP, LANES), f32),
        ],
        compiler_params=pltpu.CompilerParams(vmem_limit_bytes=56 * 1024 * 1024),
        name="strip_image",
    )(
        counts, offsets, vis, weight, kernel, tile, plane, chan,
        jnp.asarray(tap_table()), jnp.asarray(line_table()), jnp.asarray(twist_table()), jnp.asarray(screen_table()),
    )


def solve_taylor(moments, images):
    entry_00, entry_01, entry_02 = (moments[0], moments[1], moments[2])
    entry_11, entry_12, entry_22 = (moments[2], moments[3], moments[4])
    minor_00 = entry_11 * entry_22 - entry_12 * entry_12
    minor_01 = entry_02 * entry_12 - entry_01 * entry_22
    minor_02 = entry_01 * entry_12 - entry_02 * entry_11
    minor_11 = entry_00 * entry_22 - entry_02 * entry_02
    minor_12 = entry_01 * entry_02 - entry_00 * entry_12
    minor_22 = entry_00 * entry_11 - entry_01 * entry_01
    determinant = entry_00 * minor_00 + entry_01 * minor_01 + entry_02 * minor_02
    first = (minor_00 * images[0] + minor_01 * images[1] + minor_02 * images[2]) / determinant
    second = (minor_01 * images[0] + minor_11 * images[1] + minor_12 * images[2]) / determinant
    third = (minor_02 * images[0] + minor_12 * images[1] + minor_22 * images[2]) / determinant
    return jnp.stack([first, second, third])


def body(vis_value, vis_weight, kernel, tile_index, plane_index, chan_index, chan_offset, counts):
    pieces = device_image(
        counts, chan_offset, vis_value[0, 0], vis_weight[0], kernel[0, 0],
        tile_index[0], plane_index[0], chan_index[0],
    )
    pieces = pieces.reshape(4, 64 * 4, LANES)
    pieces = lax.all_to_all(pieces, CHAN, split_axis=0, concat_axis=0, tiled=True).sum(axis=0)
    pieces = pieces.reshape(64, 4, LANES)
    pieces = lax.all_to_all(pieces, BL, split_axis=0, concat_axis=0, tiled=True).sum(axis=0)
    return solve_taylor(pieces[TAYLOR, :MOMENTS], pieces[:TAYLOR])


def solution(mesh):
    split = Mesh(mesh.devices.reshape(2, 2, 4, 4, 4), ("chan_0", "chan_1", "bl_0", "bl_1", "bl_2"))
    return jax.shard_map(
        body,
        mesh=split,
        in_specs=(
            P(CHAN, BL, None, None),
            P(CHAN, BL, None),
            P(CHAN, BL, None, None),
            P(CHAN, BL, None),
            P(CHAN, BL, None),
            P(CHAN, BL, None),
            P(CHAN, None),
            P(CHAN, BL),
        ),
        out_specs=P(None, CHAN_BL),
        check_vma=False,
    )
```

time: 489 us -> 72.6 us (0.15)
  the two profiles are of different devices: /device:TPU:32 before, /device:TPU:1 now
where the time goes in v1:
time: 72.6 us; the launch traced here: 72.2 us
  blocking collectives  38.6 us (53%)
  between operations  16.5 us (23%)
  Pallas kernels  15.7 us (22%)
    all_to_all x1, blocking collectives, body(): lax.all_to_all(pieces, BL, split_axis=0, concat_axis=0, tiled=True)  24.2 us
    pallas_call x1, Pallas kernels, device_image(): pl.pallas_call(image_kernel, out_shape=jax.ShapeDtypeStruct((STRIP * BLOC...  15.7 us
    all_to_all x1, blocking collectives, body(): lax.all_to_all(pieces, CHAN, split_axis=0, concat_axis=0, tiled=True)  14.4 us

profile of v1, /device:TPU:1, one launch (start us, length us, event | category | flops | bytes accessed | tf_op | source)
XLA Modules:
  0.0 72.2 jit_solution(11937521328412733647)
XLA Ops:
  0.7 15.7 %strip_image.1 = f32[1024,128]{1,0:T(8,128)} custom-call(s32[1,1]{1,0:T(1,128)S(6)} %copy.23.count_ref, f32[1,16]{1,0:T(1,128)} %offset_ref.1, bf16[2,2048]{1,0:T(2,128)(2,1)} %bitcast.16, bf16[1,2048]{1,0:T(2,128)(2,1)} %bitcast.17, bf16[64,2048]{1,0:T(8,128)(2,1)} %bitcast.15, s32[1,2048]{1,0:T(1,128)} %bitcast.18, s32[1,2048]{1,0:T(1,128)} %bitcast.19, ...), custom_call_target="tpu_custom_call" | custom-call | tf_op jit(solution)/shard_map/strip_image/pallas_call | solution.py:286
  16.4 14.4 %all_to_all.10 = f32[4,256,128]{2,1,0:T(8,128)S(1)} all-to-all(f32[4,256,128]{2,1,0:T(8,128)} %bitcast.13), channel_id=1, replica_groups=mesh['chan_0'=2,'chan_1'=2,'bl_0'=4,'bl_1'=4,'bl_2'=4] {'chan_0','chan_1'}, dimensions={0} | all-to-all | bytes 1048576 | tf_op jit(solution)/shard_map/all_to_all | solution.py:330
  30.8 24.2 %all_to_all.11 = f32[64,4,128]{2,1,0:T(4,128)S(1)} all-to-all(f32[64,4,128]{2,1,0:T(4,128)S(1)} %bitcast.14), channel_id=1, replica_groups=mesh['chan_0'=2,'chan_1'=2,'bl_0'=4,'bl_1'=4,'bl_2'=4] {'bl_0','bl_1','b..., dimensions={0} | all-to-all | bytes 262144 | tf_op jit(solution)/shard_map/all_to_all | solution.py:332
  55.0 0.1 reduce_sum.19
  55.1 0.7 fusion
  71.6 0.6 pad_maximum_fusion
  (2 shorter events, 0.0 us)

commit v2 on v1

--- a/solution.py
+++ b/solution.py
@@ -318,7 +318,101 @@
     first = (minor_00 * images[0] + minor_01 * images[1] + minor_02 * images[2]) / determinant
     second = (minor_01 * images[0] + minor_11 * images[1] + minor_12 * images[2]) / determinant
     third = (minor_02 * images[0] + minor_12 * images[1] + minor_22 * images[2]) / determinant
-    return jnp.stack([first, second, third])
+    return first, second, third
+
+
+MESH_ID = pl.DeviceIdType.MESH
+
+
+def sum_kernel(
+    own_ref, out_ref, pair_in, pair_sum, plane_in, plane_sum, line_in,
+    pair_send, pair_recv, plane_send, plane_recv, line_send, line_recv,
+):
+    low = lax.axis_index("chan_0")
+    core = lax.axis_index("chan_1")
+    flat = lax.axis_index("bl_0") * 4 + lax.axis_index("bl_1")
+    deep = lax.axis_index("bl_2") * 2 + low
+    partner = {"chan_1": 1 - core}
+
+    def plane_peer(j):
+        there = (flat + j) % 16
+        return there, {"bl_0": there // 4, "bl_1": there % 4}
+
+    def line_peer(j):
+        there = (deep + j) % 8
+        return there, {"bl_2": there // 2, "chan_0": there % 2}
+
+    barrier = pltpu.get_barrier_semaphore()
+    pl.semaphore_signal(barrier, inc=1, device_id=partner, device_id_type=MESH_ID)
+    for j in range(1, 16):
+        pl.semaphore_signal(barrier, inc=1, device_id=plane_peer(j)[1], device_id_type=MESH_ID)
+    for j in range(1, 8):
+        pl.semaphore_signal(barrier, inc=1, device_id=line_peer(j)[1], device_id_type=MESH_ID)
+    pl.semaphore_wait(barrier, 23)
+
+    pair = pltpu.make_async_remote_copy(
+        src_ref=own_ref.at[:, 1 - core], dst_ref=pair_in, send_sem=pair_send, recv_sem=pair_recv,
+        device_id=partner, device_id_type=MESH_ID,
+    )
+    pair.start()
+    pair.wait()
+    for z in range(2):
+        pair_sum[:, z] = own_ref[z, core] + pair_in[z]
+
+    copies = []
+    for j in range(1, 16):
+        there, where = plane_peer(j)
+        copies.append(
+            pltpu.make_async_remote_copy(
+                src_ref=pair_sum.at[there], dst_ref=plane_in.at[j], send_sem=plane_send.at[j],
+                recv_sem=plane_recv.at[j], device_id=where, device_id_type=MESH_ID,
+            )
+        )
+        copies[-1].start()
+    total = pair_sum[flat]
+    for j, copy in enumerate(copies):
+        copy.wait()
+        total = total + plane_in[j + 1]
+    plane_sum[...] = total
+
+    copies = []
+    for j in range(1, 8):
+        there, where = line_peer(j)
+        copies.append(
+            pltpu.make_async_remote_copy(
+                src_ref=plane_sum.at[there % 2, there // 2], dst_ref=line_in.at[j], send_sem=line_send.at[j],
+                recv_sem=line_recv.at[j], device_id=where, device_id_type=MESH_ID,
+            )
+        )
+        copies[-1].start()
+    total = plane_sum[low, deep // 2]
+    for j, copy in enumerate(copies):
+        copy.wait()
+        total = total + line_in[j + 1]
+    moments = [total[TAYLOR:TAYLOR + 1, m:m + 1] for m in range(MOMENTS)]
+    images = [total[k:k + 1] for k in range(TAYLOR)]
+    for k, row in enumerate(solve_taylor(moments, images)):
+        out_ref[k:k + 1] = row
+
+
+def summed(pieces):
+    dma = pltpu.SemaphoreType.DMA
+    return pl.pallas_call(
+        sum_kernel,
+        out_shape=jax.ShapeDtypeStruct((TAYLOR, LANES), f32),
+        in_specs=[pl.BlockSpec(memory_space=pltpu.VMEM)],
+        out_specs=pl.BlockSpec(memory_space=pltpu.VMEM),
+        scratch_shapes=[
+            pltpu.VMEM((2, 16, 4, 4, LANES), f32),
+            pltpu.VMEM((16, 2, 4, 4, LANES), f32),
+            pltpu.VMEM((16, 2, 4, 4, LANES), f32),
+            pltpu.VMEM((2, 4, 4, LANES), f32),
+            pltpu.VMEM((8, 4, LANES), f32),
+            dma, dma, dma((16,)), dma((16,)), dma((8,)), dma((8,)),
+        ],
+        compiler_params=pltpu.CompilerParams(collective_id=0, has_side_effects=True),
+        name="sum_and_solve",
+    )(pieces.reshape(2, 2, 16, 4, 4, LANES))
 
 
 def body(vis_value, vis_weight, kernel, tile_index, plane_index, chan_index, chan_offset, counts):
@@ -326,11 +420,7 @@
         counts, chan_offset, vis_value[0, 0], vis_weight[0], kernel[0, 0],
         tile_index[0], plane_index[0], chan_index[0],
     )
-    pieces = pieces.reshape(4, 64 * 4, LANES)
-    pieces = lax.all_to_all(pieces, CHAN, split_axis=0, concat_axis=0, tiled=True).sum(axis=0)
-    pieces = pieces.reshape(64, 4, LANES)
-    pieces = lax.all_to_all(pieces, BL, split_axis=0, concat_axis=0, tiled=True).sum(axis=0)
-    return solve_taylor(pieces[TAYLOR, :MOMENTS], pieces[:TAYLOR])
+    return summed(pieces)
 
 
 def solution(mesh):

time: 72.6 us -> 41.2 us (0.57)
  blocking collectives: 38.6 us -> 0 us
  Pallas kernels: 15.7 us -> 38.7 us
  between operations: 16.5 us -> 0.66 us
    all_to_all x2 -> x0, blocking collectives: 38.6 us -> none  [the longest x1 24.2 us: body(): lax.all_to_all(pieces, BL, split_axis=0, concat_axis=0, tiled=True)]
    pallas_call x0 -> x1, Pallas kernels: none -> 23 us  [summed(): pl.pallas_call(sum_kernel, out_shape=jax.ShapeDtypeStruct((TAYLOR, LANES)...]
    unnamed x0 -> x1, local copies, waits for them, and re-layouts: none -> 1.26 us
where the time goes in v2:
time: 41.2 us; the launch traced here: 40.6 us
  Pallas kernels  38.7 us (94%)
  local copies, waits for them, and re-layouts  1.26 us (3%)
  between operations  0.66 us (2%)
    pallas_call x1, Pallas kernels, summed(): pl.pallas_call(sum_kernel, out_shape=jax.ShapeDtypeStruct((TAYLOR, LANES)...  23 us
    pallas_call x1, Pallas kernels, device_image(): pl.pallas_call(image_kernel, out_shape=jax.ShapeDtypeStruct((STRIP * BLOC...  15.7 us
    unnamed x1, local copies, waits for them, and re-layouts  1.26 us

profile of v2, /device:TPU:1, one launch (start us, length us, event | category | flops | bytes accessed | tf_op | source)
XLA Modules:
  0.0 40.6 jit_solution(1238018804858183308)
XLA Ops:
  0.7 15.7 %strip_image.1 = f32[1024,128]{1,0:T(8,128)} custom-call(s32[1,1]{1,0:T(1,128)S(6)} %copy.14.count_ref, f32[1,16]{1,0:T(1,128)} %offset_ref.1, bf16[2,2048]{1,0:T(2,128)(2,1)} %bitcast.9, bf16[1,2048]{1,0:T(2,128)(2,1)} %bitcast.10, bf16[64,2048]{1,0:T(8,128)(2,1)} %bitcast.8, s32[1,2048]{1,0:T(1,128)} %bitcast.11, s32[1,2048]{1,0:T(1,128)} %bitcast.12, ...), custom_call_target="tpu_custom_call" | custom-call | tf_op jit(solution)/shard_map/strip_image/pallas_call | solution.py:286
  16.4 23.0 %sum_and_solve.1 = f32[3,128]{1,0:T(4,128)} custom-call(f32[2,2,16,4,4,128]{5,4,3,2,1,0:T(4,128)} %bitcast.7), custom_call_target="tpu_custom_call" | custom-call | tf_op jit(solution)/shard_map/sum_and_solve/pallas_call | solution.py:400
  39.4 1.3 %copy.15 = f32[3,128]{1,0:T(4,128)} copy(f32[3,128]{1,0:T(4,128)} %sum_and_solve.1) | data formatting | bytes 3072

commit v3 on v1

--- a/solution.py
+++ b/solution.py
@@ -128,8 +128,22 @@
 
 def image_kernel(
     count_ref, offset_ref, vis_ref, weight_ref, kernel_ref, tile_ref, plane_ref, chan_ref,
-    tap_ref, line_ref, twist_ref, screen_ref, out_ref, taps, updates, cell_of, grid, lines, screens, image,
+    tap_ref, line_ref, twist_ref, screen_ref, out_ref, taps, updates, bank_of, lane_hot, hot, grid, lines, screens, image,
+    own, pair_in, pair_sum, plane_in, plane_sum, line_in, moment_own, moment_in, moment_pair,
+    pair_send, pair_recv, moment_sem, plane_send, plane_recv, line_send, line_recv,
 ):
+    barrier = pltpu.get_barrier_semaphore()
+    signal = functools.partial(pl.semaphore_signal, barrier, inc=1, device_id_type=MESH_ID)
+    signal(device_id={"chan_1": 1 - lax.axis_index("chan_1")})
+    flat = lax.axis_index("bl_0") * 4 + lax.axis_index("bl_1")
+    for j in range(1, 16):
+        there = (flat + j) % 16
+        signal(device_id={"bl_0": there // 4, "bl_1": there % 4})
+    deep = lax.axis_index("chan_0") * 4 + lax.axis_index("bl_2")
+    for j in range(1, 8):
+        there = (deep + j) % 8
+        signal(device_id={"bl_2": there % 4, "chan_0": there // 4})
+
     taps[...] = jnp.dot(tap_ref[...], kernel_ref[...], preferred_element_type=f32)
     count = count_ref[0, 0]
 
@@ -147,8 +161,10 @@
         tile_v = tile & 511
         tile_v = jnp.where(direct, tile_v, 511 - tile_v)
         half = jnp.where(direct, plane - HALF_PLANES, HALF_PLANES - 1 - plane)
-        cell = half * 512 + (tile_v & 3) * LANES + (tile_v >> 2)
-        cell_of[at, :] = jnp.transpose(jnp.broadcast_to(cell.astype(f32), (LANES, CHUNK)))
+        across = lambda row: jnp.transpose(jnp.broadcast_to(row.astype(f32), (LANES, CHUNK)))
+        bank_of[at, :] = across(half * 4 + (tile_v & 3)).astype(bf16)
+        lane = lax.broadcasted_iota(jnp.int32, (CHUNK, LANES), 1).astype(f32)
+        lane_hot[at, :] = jnp.where(across(tile_v >> 2) == lane, 1.0, 0.0).astype(bf16)
         weighted = weight * taps[256:257, at]
         new_sums = []
         power = weighted
@@ -198,23 +214,28 @@
     for m in range(MOMENTS):
         total = jnp.sum(sums[m], axis=1, keepdims=True)
         moment_row = jnp.where(lane == m, jnp.broadcast_to(total, (STRIP, LANES)), moment_row)
-
-    def one_stretch(step, carry):
-        first = step * CHUNK
-        cells = cell_of[...]
-        pos = lax.broadcasted_iota(jnp.int32, (1, LANES), 1) + first
-        hot = jnp.concatenate(
-            [
-                jnp.where(cells == (pos + half * LANES).astype(f32), 1.0, 0.0).astype(bf16)
-                for half in range(CHUNK // LANES)
-            ],
-            axis=1,
-        )
-        both = jnp.dot(updates[...], hot, preferred_element_type=f32)
-        grid[:, pl.ds(pl.multiple_of(first, CHUNK), CHUNK)] = both[:ROWS] + both[ROWS:]
+    moment_own[...] = moment_row
+
+    def fill(step, slot):
+        banks = bank_of[...]
+        for half in range(CHUNK // LANES):
+            bank = (step * (CHUNK // LANES) + half).astype(f32).astype(bf16)
+            hot[slot, :, half * LANES:(half + 1) * LANES] = jnp.where(banks == bank, lane_hot[...], jnp.zeros((), bf16))
+
+    def spread(step, slot):
+        both = jnp.dot(updates[...], hot[slot], preferred_element_type=f32)
+        grid[:, pl.ds(pl.multiple_of(step * CHUNK, CHUNK), CHUNK)] = both[:ROWS] + both[ROWS:]
+
+    def two_stretches(turn, carry):
+        step = turn * 2
+        spread(step, 0)
+        fill(step + 1, 1)
+        spread(step + 1, 1)
+        fill(step + 2, 0)
         return carry
 
-    lax.fori_loop(0, CELLS // CHUNK, one_stretch, 0)
+    fill(jnp.int32(0), 0)
+    lax.fori_loop(0, CELLS // CHUNK // 2, two_stretches, 0)
 
     for b in range(BLOCKS):
         one = (screen_ref[0, b], screen_ref[1, b])
@@ -230,8 +251,8 @@
         at = pl.ds(pl.multiple_of(q * 512 + vb * LANES, LANES), LANES)
         return grid[first:first + STRIP, at]
 
-    def one_plane(q, carry):
-        for k in range(TAYLOR):
+    def one_term(k):
+        for q in range(HALF_PLANES):
             residues = []
             for vb in range(4):
                 halves = []
@@ -246,17 +267,18 @@
             whole = jnp.concatenate(residues, axis=0)
             high = whole.astype(bf16)
             low = (whole - high.astype(f32)).astype(bf16)
-            lines[...] = (
+            lines[q] = (
                 jnp.dot(high, line_ref[0:256], preferred_element_type=f32)
                 + jnp.dot(low, line_ref[0:256], preferred_element_type=f32)
                 + jnp.dot(high, line_ref[256:512], preferred_element_type=f32)
             )
+        for q in range(HALF_PLANES):
             quarters = [[], [], [], []]
             for e in range(TILE):
                 x = []
                 for vb in range(4):
                     first = (vb * TILE + e) * STRIP
-                    value = (lines[first:first + STRIP, 0:LANES], lines[first:first + STRIP, LANES:2 * LANES])
+                    value = (lines[q, first:first + STRIP, 0:LANES], lines[q, first:first + STRIP, LANES:2 * LANES])
                     if vb > 0:
                         value = cmul(value, (twist_ref[vb:vb + 1], twist_ref[36 + vb:37 + vb]))
                     x.append(value)
@@ -269,35 +291,134 @@
                 for mh, value in enumerate(eight_point(quarters[mr])):
                     b = 4 * mh + mr
                     add = value[0] * screens[q, 0, b] - value[1] * screens[q, 1, b]
-                    image[k, b] = image[k, b] + add
-        return carry
-
-    image[...] = jnp.zeros_like(image)
-    lax.fori_loop(0, HALF_PLANES, one_plane, 0)
-    for b in range(BLOCKS):
-        for k in range(TAYLOR):
-            out_ref[pl.ds(b * 4 + k, STRIP, stride=LANES), :] = image[k, b]
-        out_ref[pl.ds(b * 4 + TAYLOR, STRIP, stride=LANES), :] = moment_row
+                    if q < HALF_PLANES - 1:
+                        image[b] = image[b] + add if q > 0 else add
+                    else:
+                        own[k, pl.ds(b, STRIP, stride=BLOCKS), :] = image[b] + add
+
+    low_z = lax.axis_index("chan_0")
+    core = lax.axis_index("chan_1")
+    flat = lax.axis_index("bl_0") * 4 + lax.axis_index("bl_1")
+    deep = low_z * 4 + lax.axis_index("bl_2")
+
+    def pair_copies(k):
+        return [
+            pltpu.make_async_remote_copy(
+                src_ref=own.at[k, pl.ds(pl.multiple_of(z * 128 + (1 - core) * 64, 64), 64)],
+                dst_ref=pair_in.at[k, pl.ds(z * 64, 64)],
+                send_sem=pair_send.at[k, z], recv_sem=pair_recv.at[k, z],
+                device_id={"chan_1": 1 - core}, device_id_type=MESH_ID,
+            )
+            for z in range(2)
+        ]
+
+    def moment_copy():
+        return pltpu.make_async_remote_copy(
+            src_ref=moment_own, dst_ref=moment_in, send_sem=moment_sem.at[0], recv_sem=moment_sem.at[1],
+            device_id={"chan_1": 1 - core}, device_id_type=MESH_ID,
+        )
+
+    def plane_copies(k):
+        copies = []
+        for j in range(1, 16):
+            there = (flat + j) % 16
+            copies.append(
+                pltpu.make_async_remote_copy(
+                    src_ref=pair_sum.at[k, there] if k < TAYLOR else moment_pair,
+                    dst_ref=plane_in.at[k, j], send_sem=plane_send.at[k, j], recv_sem=plane_recv.at[k, j],
+                    device_id={"bl_0": there // 4, "bl_1": there % 4}, device_id_type=MESH_ID,
+                )
+            )
+        return copies
+
+    def join_pair(k):
+        for copy in pair_copies(k):
+            copy.wait()
+        sums = [
+            own[k, pl.ds(pl.multiple_of(z * 128 + core * 64, 64), 64)] + pair_in[k, z * 64:z * 64 + 64] for z in range(2)
+        ]
+        for xy in range(16):
+            pair_sum[k, xy] = jnp.concatenate([sums[z][xy * 4:xy * 4 + 4] for z in range(2)], axis=0)
+        for copy in plane_copies(k):
+            copy.start()
+
+    for k in range(TAYLOR):
+        one_term(k)
+        if k == 0:
+            pl.semaphore_wait(barrier, 23)
+            moment_copy().start()
+        for copy in pair_copies(k):
+            copy.start()
+        if k == 0:
+            moment_copy().wait()
+            moment_pair[...] = moment_own[...] + moment_in[...]
+            for copy in plane_copies(TAYLOR):
+                copy.start()
+        else:
+            join_pair(k - 1)
+    join_pair(TAYLOR - 1)
+
+    for k in (TAYLOR, 0, 1, 2):
+        total = pair_sum[k, flat] if k < TAYLOR else moment_pair[...]
+        for j, copy in enumerate(plane_copies(k)):
+            copy.wait()
+            total = total + plane_in[k, j + 1]
+        for r in range(8):
+            plane_sum[r, k:k + 1] = total[r:r + 1]
+
+    copies = []
+    for j in range(1, 8):
+        there = (deep + j) % 8
+        copies.append(
+            pltpu.make_async_remote_copy(
+                src_ref=plane_sum.at[there], dst_ref=line_in.at[j], send_sem=line_send.at[j],
+                recv_sem=line_recv.at[j], device_id={"bl_2": there % 4, "chan_0": there // 4}, device_id_type=MESH_ID,
+            )
+        )
+        copies[-1].start()
+    total = plane_sum[deep]
+    for j, copy in enumerate(copies):
+        copy.wait()
+        total = total + line_in[j + 1]
+    moments = [total[TAYLOR:TAYLOR + 1, m:m + 1] for m in range(MOMENTS)]
+    images = [total[k:k + 1] for k in range(TAYLOR)]
+    for k, row in enumerate(solve_taylor(moments, images)):
+        out_ref[k:k + 1] = row
 
 
 def device_image(counts, offsets, vis, weight, kernel, tile, plane, chan):
     smem = pl.BlockSpec(memory_space=pltpu.SMEM)
     vmem = pl.BlockSpec(memory_space=pltpu.VMEM)
+    dma = pltpu.SemaphoreType.DMA
     return pl.pallas_call(
         image_kernel,
-        out_shape=jax.ShapeDtypeStruct((STRIP * BLOCKS * 4, LANES), f32),
+        out_shape=jax.ShapeDtypeStruct((TAYLOR, LANES), f32),
         in_specs=[smem, smem] + [vmem] * 10,
         out_specs=vmem,
         scratch_shapes=[
             pltpu.VMEM((272, SLOTS), f32),
             pltpu.VMEM((2 * ROWS, SLOTS), bf16),
-            pltpu.VMEM((SLOTS, LANES), f32),
+            pltpu.VMEM((SLOTS, LANES), bf16),
+            pltpu.VMEM((SLOTS, LANES), bf16),
+            pltpu.VMEM((2, SLOTS, CHUNK), bf16),
             pltpu.VMEM((ROWS, CELLS), f32),
-            pltpu.VMEM((256, 256), f32),
+            pltpu.VMEM((HALF_PLANES, 256, 256), f32),
             pltpu.VMEM((HALF_PLANES, 2, BLOCKS, STRIP, LANES), f32),
-            pltpu.VMEM((TAYLOR, BLOCKS, STRIP, LANES), f32),
+            pltpu.VMEM((BLOCKS, STRIP, LANES), f32),
+            pltpu.VMEM((TAYLOR, 256, LANES), f32),
+            pltpu.VMEM((TAYLOR, 128, LANES), f32),
+            pltpu.VMEM((TAYLOR, 16, 8, LANES), f32),
+            pltpu.VMEM((TAYLOR + 1, 16, 8, LANES), f32),
+            pltpu.VMEM((8, 4, LANES), f32),
+            pltpu.VMEM((8, 4, LANES), f32),
+            pltpu.VMEM((8, LANES), f32),
+            pltpu.VMEM((8, LANES), f32),
+            pltpu.VMEM((8, LANES), f32),
+            dma((TAYLOR, 2)), dma((TAYLOR, 2)), dma((2,)), dma((4, 16)), dma((4, 16)), dma((8,)), dma((8,)),
         ],
-        compiler_params=pltpu.CompilerParams(vmem_limit_bytes=56 * 1024 * 1024),
+        compiler_params=pltpu.CompilerParams(
+            vmem_limit_bytes=56 * 1024 * 1024, collective_id=0, has_side_effects=True
+        ),
         name="strip_image",
     )(
         counts, offsets, vis, weight, kernel, tile, plane, chan,
@@ -318,19 +439,17 @@
     first = (minor_00 * images[0] + minor_01 * images[1] + minor_02 * images[2]) / determinant
     second = (minor_01 * images[0] + minor_11 * images[1] + minor_12 * images[2]) / determinant
     third = (minor_02 * images[0] + minor_12 * images[1] + minor_22 * images[2]) / determinant
-    return jnp.stack([first, second, third])
+    return first, second, third
+
+
+MESH_ID = pl.DeviceIdType.MESH
 
 
 def body(vis_value, vis_weight, kernel, tile_index, plane_index, chan_index, chan_offset, counts):
-    pieces = device_image(
+    return device_image(
         counts, chan_offset, vis_value[0, 0], vis_weight[0], kernel[0, 0],
         tile_index[0], plane_index[0], chan_index[0],
     )
-    pieces = pieces.reshape(4, 64 * 4, LANES)
-    pieces = lax.all_to_all(pieces, CHAN, split_axis=0, concat_axis=0, tiled=True).sum(axis=0)
-    pieces = pieces.reshape(64, 4, LANES)
-    pieces = lax.all_to_all(pieces, BL, split_axis=0, concat_axis=0, tiled=True).sum(axis=0)
-    return solve_taylor(pieces[TAYLOR, :MOMENTS], pieces[:TAYLOR])
 
 
 def solution(mesh):

time: 72.6 us -> 38 us (0.52)
  blocking collectives: 38.6 us -> 0 us
  Pallas kernels: 15.7 us -> 36 us
  between operations: 16.5 us -> 0.66 us
    all_to_all x2 -> x0, blocking collectives: 38.6 us -> none  [the longest x1 24.2 us: body(): lax.all_to_all(pieces, BL, split_axis=0, concat_axis=0, tiled=True)]
    pallas_call x1, Pallas kernels: 15.7 us -> 36 us  [device_image(): pl.pallas_call(image_kernel, out_shape=jax.ShapeDtypeStruct((TAYLOR, LANE...]
    unnamed x0 -> x1, local copies, waits for them, and re-layouts: none -> 1.26 us
where the time goes in v3:
time: 38 us; the launch traced here: 37.9 us
  Pallas kernels  36 us (95%)
  local copies, waits for them, and re-layouts  1.26 us (3%)
  between operations  0.66 us (2%)
    pallas_call x1, Pallas kernels, device_image(): pl.pallas_call(image_kernel, out_shape=jax.ShapeDtypeStruct((TAYLOR, LANE...  36 us
    unnamed x1, local copies, waits for them, and re-layouts  1.26 us

profile of v3, /device:TPU:1, one launch (start us, length us, event | category | flops | bytes accessed | tf_op | source)
XLA Modules:
  0.0 37.9 jit_solution(2167136001979074068)
XLA Ops:
  0.7 36.0 %strip_image.1 = f32[3,128]{1,0:T(4,128)} custom-call(s32[1,1]{1,0:T(1,128)S(6)} %copy.14.count_ref, f32[1,16]{1,0:T(1,128)} %offset_ref.1, bf16[2,2048]{1,0:T(2,128)(2,1)} %bitcast.7, bf16[1,2048]{1,0:T(2,128)(2,1)} %bitcast.8, bf16[64,2048]{1,0:T(8,128)(2,1)} %bitcast.6, s32[1,2048]{1,0:T(1,128)} %bitcast.9, s32[1,2048]{1,0:T(1,128)} %bitcast.10, ...), custom_call_target="tpu_custom_call" | custom-call | tf_op jit(solution)/shard_map/strip_image/pallas_call | solution.py:393
  36.6 1.3 %copy.15 = f32[3,128]{1,0:T(4,128)} copy(f32[3,128]{1,0:T(4,128)} %strip_image.1) | data formatting | bytes 3072

commit v4 on v3

--- a/solution.py
+++ b/solution.py
@@ -128,7 +128,7 @@
 
 def image_kernel(
     count_ref, offset_ref, vis_ref, weight_ref, kernel_ref, tile_ref, plane_ref, chan_ref,
-    tap_ref, line_ref, twist_ref, screen_ref, out_ref, taps, updates, bank_of, lane_hot, hot, grid, lines, screens, image,
+    tap_ref, line_ref, twist_ref, screen_ref, out_ref, taps, updates, bank_of, lane_hot, grid, lines, screens, image,
     own, pair_in, pair_sum, plane_in, plane_sum, line_in, moment_own, moment_in, moment_pair,
     pair_send, pair_recv, moment_sem, plane_send, plane_recv, line_send, line_recv,
 ):
@@ -145,7 +145,8 @@
         signal(device_id={"bl_2": there % 4, "chan_0": there // 4})
 
     taps[...] = jnp.dot(tap_ref[...], kernel_ref[...], preferred_element_type=f32)
-    count = count_ref[0, 0]
+    count = jnp.broadcast_to(count_ref[0:1, 0:1], (1, CHUNK))
+    offsets = [jnp.broadcast_to(offset_ref[0:1, c:c + 1], (1, CHUNK)) for c in range(16)]
 
     def one_chunk(step, sums):
         at = pl.ds(pl.multiple_of(step * CHUNK, CHUNK), CHUNK)
@@ -154,7 +155,7 @@
         chan = chan_ref[:, at]
         coord = jnp.zeros((1, CHUNK), f32)
         for c in range(16):
-            coord = jnp.where(chan == c, offset_ref[0, c], coord)
+            coord = jnp.where(chan == c, offsets[c], coord)
         tile = tile_ref[:, at]
         plane = plane_ref[:, at]
         direct = plane >= HALF_PLANES
@@ -216,26 +217,14 @@
         moment_row = jnp.where(lane == m, jnp.broadcast_to(total, (STRIP, LANES)), moment_row)
     moment_own[...] = moment_row
 
-    def fill(step, slot):
+    for step in range(CELLS // CHUNK):
         banks = bank_of[...]
-        for half in range(CHUNK // LANES):
-            bank = (step * (CHUNK // LANES) + half).astype(f32).astype(bf16)
-            hot[slot, :, half * LANES:(half + 1) * LANES] = jnp.where(banks == bank, lane_hot[...], jnp.zeros((), bf16))
-
-    def spread(step, slot):
-        both = jnp.dot(updates[...], hot[slot], preferred_element_type=f32)
-        grid[:, pl.ds(pl.multiple_of(step * CHUNK, CHUNK), CHUNK)] = both[:ROWS] + both[ROWS:]
-
-    def two_stretches(turn, carry):
-        step = turn * 2
-        spread(step, 0)
-        fill(step + 1, 1)
-        spread(step + 1, 1)
-        fill(step + 2, 0)
-        return carry
-
-    fill(jnp.int32(0), 0)
-    lax.fori_loop(0, CELLS // CHUNK // 2, two_stretches, 0)
+        halves = [
+            jnp.where(banks == jnp.asarray(step * 2 + half, bf16), lane_hot[...], jnp.zeros((), bf16))
+            for half in range(CHUNK // LANES)
+        ]
+        both = jnp.dot(updates[...], jnp.concatenate(halves, axis=1), preferred_element_type=f32)
+        grid[:, step * CHUNK:(step + 1) * CHUNK] = both[:ROWS] + both[ROWS:]
 
     for b in range(BLOCKS):
         one = (screen_ref[0, b], screen_ref[1, b])
@@ -301,12 +290,18 @@
     flat = lax.axis_index("bl_0") * 4 + lax.axis_index("bl_1")
     deep = low_z * 4 + lax.axis_index("bl_2")
 
+    def together(source, target, send, recv):
+        return pltpu.make_async_remote_copy(
+            src_ref=source, dst_ref=target, send_sem=send, recv_sem=recv,
+            device_id={"chan_1": 1 - core}, device_id_type=MESH_ID,
+        )
+
     def pair_copies(k):
         return [
             pltpu.make_async_remote_copy(
                 src_ref=own.at[k, pl.ds(pl.multiple_of(z * 128 + (1 - core) * 64, 64), 64)],
                 dst_ref=pair_in.at[k, pl.ds(z * 64, 64)],
-                send_sem=pair_send.at[k, z], recv_sem=pair_recv.at[k, z],
+                send_sem=pair_send.at[k], recv_sem=pair_recv.at[k],
                 device_id={"chan_1": 1 - core}, device_id_type=MESH_ID,
             )
             for z in range(2)
@@ -325,15 +320,14 @@
             copies.append(
                 pltpu.make_async_remote_copy(
                     src_ref=pair_sum.at[k, there] if k < TAYLOR else moment_pair,
-                    dst_ref=plane_in.at[k, j], send_sem=plane_send.at[k, j], recv_sem=plane_recv.at[k, j],
+                    dst_ref=plane_in.at[k, j], send_sem=plane_send.at[k], recv_sem=plane_recv.at[k],
                     device_id={"bl_0": there // 4, "bl_1": there % 4}, device_id_type=MESH_ID,
                 )
             )
         return copies
 
     def join_pair(k):
-        for copy in pair_copies(k):
-            copy.wait()
+        together(own.at[k, 0:128], pair_in.at[k], pair_send.at[k], pair_recv.at[k]).wait()
         sums = [
             own[k, pl.ds(pl.multiple_of(z * 128 + core * 64, 64), 64)] + pair_in[k, z * 64:z * 64 + 64] for z in range(2)
         ]
@@ -360,47 +354,43 @@
 
     for k in (TAYLOR, 0, 1, 2):
         total = pair_sum[k, flat] if k < TAYLOR else moment_pair[...]
-        for j, copy in enumerate(plane_copies(k)):
-            copy.wait()
-            total = total + plane_in[k, j + 1]
+        together(pair_sum.at[0, 0:15], plane_in.at[k, 1:16], plane_send.at[k], plane_recv.at[k]).wait()
+        for j in range(1, 16):
+            total = total + plane_in[k, j]
         for r in range(8):
             plane_sum[r, k:k + 1] = total[r:r + 1]
 
-    copies = []
     for j in range(1, 8):
         there = (deep + j) % 8
-        copies.append(
-            pltpu.make_async_remote_copy(
-                src_ref=plane_sum.at[there], dst_ref=line_in.at[j], send_sem=line_send.at[j],
-                recv_sem=line_recv.at[j], device_id={"bl_2": there % 4, "chan_0": there // 4}, device_id_type=MESH_ID,
-            )
-        )
-        copies[-1].start()
+        pltpu.make_async_remote_copy(
+            src_ref=plane_sum.at[there], dst_ref=line_in.at[j], send_sem=line_send, recv_sem=line_recv,
+            device_id={"bl_2": there % 4, "chan_0": there // 4}, device_id_type=MESH_ID,
+        ).start()
     total = plane_sum[deep]
-    for j, copy in enumerate(copies):
-        copy.wait()
-        total = total + line_in[j + 1]
+    together(plane_sum.at[0:7], line_in.at[1:8], line_send, line_recv).wait()
+    for j in range(1, 8):
+        total = total + line_in[j]
     moments = [total[TAYLOR:TAYLOR + 1, m:m + 1] for m in range(MOMENTS)]
     images = [total[k:k + 1] for k in range(TAYLOR)]
-    for k, row in enumerate(solve_taylor(moments, images)):
-        out_ref[k:k + 1] = row
+    rows, determinant = solve_taylor(moments, images)
+    for k in range(TAYLOR):
+        out_ref[0, k:k + 1] = rows[k]
+        out_ref[1, k:k + 1] = jnp.broadcast_to(determinant, (1, LANES))
 
 
 def device_image(counts, offsets, vis, weight, kernel, tile, plane, chan):
-    smem = pl.BlockSpec(memory_space=pltpu.SMEM)
     vmem = pl.BlockSpec(memory_space=pltpu.VMEM)
     dma = pltpu.SemaphoreType.DMA
     return pl.pallas_call(
         image_kernel,
-        out_shape=jax.ShapeDtypeStruct((TAYLOR, LANES), f32),
-        in_specs=[smem, smem] + [vmem] * 10,
+        out_shape=jax.ShapeDtypeStruct((2, TAYLOR, LANES), f32),
+        in_specs=[vmem] * 12,
         out_specs=vmem,
         scratch_shapes=[
             pltpu.VMEM((272, SLOTS), f32),
             pltpu.VMEM((2 * ROWS, SLOTS), bf16),
             pltpu.VMEM((SLOTS, LANES), bf16),
             pltpu.VMEM((SLOTS, LANES), bf16),
-            pltpu.VMEM((2, SLOTS, CHUNK), bf16),
             pltpu.VMEM((ROWS, CELLS), f32),
             pltpu.VMEM((HALF_PLANES, 256, 256), f32),
             pltpu.VMEM((HALF_PLANES, 2, BLOCKS, STRIP, LANES), f32),
@@ -414,10 +404,10 @@
             pltpu.VMEM((8, LANES), f32),
             pltpu.VMEM((8, LANES), f32),
             pltpu.VMEM((8, LANES), f32),
-            dma((TAYLOR, 2)), dma((TAYLOR, 2)), dma((2,)), dma((4, 16)), dma((4, 16)), dma((8,)), dma((8,)),
+            dma((3,)), dma((3,)), dma((2,)), dma((4,)), dma((4,)), dma, dma,
         ],
         compiler_params=pltpu.CompilerParams(
-            vmem_limit_bytes=56 * 1024 * 1024, collective_id=0, has_side_effects=True
+            vmem_limit_bytes=40 * 1024 * 1024, collective_id=0, has_side_effects=True
         ),
         name="strip_image",
     )(
@@ -436,20 +426,21 @@
     minor_12 = entry_01 * entry_02 - entry_00 * entry_12
     minor_22 = entry_00 * entry_11 - entry_01 * entry_01
     determinant = entry_00 * minor_00 + entry_01 * minor_01 + entry_02 * minor_02
-    first = (minor_00 * images[0] + minor_01 * images[1] + minor_02 * images[2]) / determinant
-    second = (minor_01 * images[0] + minor_11 * images[1] + minor_12 * images[2]) / determinant
-    third = (minor_02 * images[0] + minor_12 * images[1] + minor_22 * images[2]) / determinant
-    return first, second, third
+    first = minor_00 * images[0] + minor_01 * images[1] + minor_02 * images[2]
+    second = minor_01 * images[0] + minor_11 * images[1] + minor_12 * images[2]
+    third = minor_02 * images[0] + minor_12 * images[1] + minor_22 * images[2]
+    return (first, second, third), determinant
 
 
 MESH_ID = pl.DeviceIdType.MESH
 
 
 def body(vis_value, vis_weight, kernel, tile_index, plane_index, chan_index, chan_offset, counts):
-    return device_image(
+    scaled = device_image(
         counts, chan_offset, vis_value[0, 0], vis_weight[0], kernel[0, 0],
         tile_index[0], plane_index[0], chan_index[0],
     )
+    return scaled[0] / scaled[1]
 
 
 def solution(mesh):

time: 38 us -> 40.8 us (1.074)
  local copies, waits for them, and re-layouts: 1.26 us -> 7.93 us
  Pallas kernels: 36 us -> 31.1 us
  other arithmetic: 0 us -> 0.59 us
    unnamed x1 -> x22, local copies, waits for them, and re-layouts: 1.26 us -> 7.93 us
    pallas_call x1, Pallas kernels: 36 us -> 31.1 us  [device_image(): pl.pallas_call(image_kernel, out_shape=jax.ShapeDtypeStruct((2, TAYLOR, L...]
    div x0 -> x1, other arithmetic: none -> 0.59 us  [body(): return scaled[0] / scaled[1]]
where the time goes in v4:
time: 40.8 us; the launch traced here: 40.3 us
  Pallas kernels  31.1 us (76%)
  local copies, waits for them, and re-layouts  7.93 us (19%)
  between operations  0.69 us (2%)
  other arithmetic  0.59 us (1%)
    pallas_call x1, Pallas kernels, device_image(): pl.pallas_call(image_kernel, out_shape=jax.ShapeDtypeStruct((2, TAYLOR, L...  31.1 us
    unnamed x22, local copies, waits for them, and re-layouts  7.93 us

profile of v4, /device:TPU:1, one launch (start us, length us, event | category | flops | bytes accessed | tf_op | source)
XLA Modules:
  0.0 40.3 jit_solution(3157493412219671606)
XLA Ops:
  0.0 0.0 copy-start.5
  0.7 0.0 copy-start.10
  0.7 0.0 copy-done.5
  0.7 0.6 %copy-done.10 = f32[1,16]{1,0:T(1,128)S(1)} copy-done((f32[1,16]{1,0:T(1,128)S(1)}, f32[1,16]{1,0:T(1,128)}, u32[]{:S(2)}) %copy-start.10) | copy-done | bytes 88
  1.3 0.0 copy-start
  1.3 0.9 %copy-done = bf16[1,1,64,2048]{3,2,1,0:T(8,128)(2,1)S(1)} copy-done((bf16[1,1,64,2048]{3,2,1,0:T(8,128)(2,1)S(1)}, bf16[1,1,64,2048]{3,2,1,0:T(8,128)(2,1)}, u32[]{:S(2)}) %copy-start) | copy-done | bytes 262168
  2.3 0.0 copy-start.1
  2.3 0.9 %copy-done.1 = f32[2,32,8,128]{3,2,1,0:T(8,128)S(1)} copy-done((f32[2,32,8,128]{3,2,1,0:T(8,128)S(1)}, f32[2,32,8,128]{3,2,1,0:T(8,128)}, u32[]{:S(2)}) %copy-start.1) | copy-done | bytes 262168
  3.2 0.0 copy-start.2
  3.2 0.9 %copy-done.2 = bf16[512,256]{1,0:T(8,128)(2,1)S(1)} copy-done((bf16[512,256]{1,0:T(8,128)(2,1)S(1)}, bf16[512,256]{1,0:T(8,128)(2,1)}, u32[]{:S(2)}) %copy-start.2) | copy-done | bytes 262168
  4.2 0.0 copy-start.3
  4.2 0.9 %copy-done.3 = bf16[272,64]{1,0:T(8,128)(2,1)S(1)} copy-done((bf16[272,64]{1,0:T(8,128)(2,1)S(1)}, bf16[272,64]{1,0:T(8,128)(2,1)}, u32[]{:S(2)}) %copy-start.3) | copy-done | bytes 34840
  5.1 0.0 copy-start.4
  5.1 0.8 %copy-done.4 = f32[72,128]{1,0:T(8,128)S(1)} copy-done((f32[72,128]{1,0:T(8,128)S(1)}, f32[72,128]{1,0:T(8,128)}, u32[]{:S(2)}) %copy-start.4) | copy-done | bytes 36888
  5.8 0.0 copy-start.6
  5.8 0.7 %copy-done.6 = bf16[1,1,2048]{2,1,0:T(2,128)(2,1)S(1)} copy-done((bf16[1,1,2048]{2,1,0:T(2,128)(2,1)S(1)}, bf16[1,1,2048]{2,1,0:T(2,128)(2,1)}, u32[]{:S(2)}) %copy-start.6) | copy-done | bytes 4120
  6.5 0.0 copy-start.7
  6.5 0.7 %copy-done.7 = s32[1,1,2048]{2,1,0:T(1,128)S(1)} copy-done((s32[1,1,2048]{2,1,0:T(1,128)S(1)}, s32[1,1,2048]{2,1,0:T(1,128)}, u32[]{:S(2)}) %copy-start.7) | copy-done | bytes 8216
  7.2 0.0 copy-start.8
  7.2 0.7 %copy-done.8 = s32[1,1,2048]{2,1,0:T(1,128)S(1)} copy-done((s32[1,1,2048]{2,1,0:T(1,128)S(1)}, s32[1,1,2048]{2,1,0:T(1,128)}, u32[]{:S(2)}) %copy-start.8) | copy-done | bytes 8216
  7.9 0.0 copy-start.9
  7.9 0.7 %copy-done.9 = s32[1,1,2048]{2,1,0:T(1,128)S(1)} copy-done((s32[1,1,2048]{2,1,0:T(1,128)S(1)}, s32[1,1,2048]{2,1,0:T(1,128)}, u32[]{:S(2)}) %copy-start.9) | copy-done | bytes 8216
  8.6 31.1 %strip_image.1 = f32[2,3,128]{2,1,0:T(4,128)S(1)} custom-call(s32[1,1]{1,0:T(1,128)S(6)} %copy.13.count_ref, f32[1,16]{1,0:T(1,128)S(1)} %copy-done.10, bf16[2,2048]{1,0:T(2,128)(2,1)S(1)} %bitcast.9, bf16[1,2048]{1,0:T(2,128)(2,1)S(1)} %bitcast.10, bf16[64,2048]{1,0:T(8,128)(2,1)S(1)} %bitcast.8, s32[1,2048]{1,0:T(1,128)S(1)} %bitcast.11, ...), custom_call_target="tpu_custom_call" | custom-call | tf_op jit(solution)/shard_map/strip_image/pallas_call | solution.py:384
  39.7 0.6 %fusion = f32[3,128]{1,0:T(4,128)} fusion(f32[2,3,128]{2,1,0:T(4,128)S(1)} %strip_image.1), kind=kLoop, calls=%fused_computation.1 | loop fusion | flops 384 | bytes 4608 | tf_op jit(solution)/shard_map/div | solution.py:443
Async XLA Ops:
  0.0 0.7 %copy-start.5 = (bf16[1,1,2,2048]{3,2,1,0:T(2,128)(2,1)S(1)}, bf16[1,1,2,2048]{3,2,1,0:T(2,128)(2,1)}, u32[]{:S(2)}) copy-start(bf16[1,1,2,2048]{3,2,1,0:T(2,128)(2,1)} %param.12) | copy-start | bytes 24580
  0.7 0.7 %copy-start.10 = (f32[1,16]{1,0:T(1,128)S(1)}, f32[1,16]{1,0:T(1,128)}, u32[]{:S(2)}) copy-start(f32[1,16]{1,0:T(1,128)} %offset_ref.1) | copy-start | bytes 196
  1.3 0.9 %copy-start = (bf16[1,1,64,2048]{3,2,1,0:T(8,128)(2,1)S(1)}, bf16[1,1,64,2048]{3,2,1,0:T(8,128)(2,1)}, u32[]{:S(2)}) copy-start(bf16[1,1,64,2048]{3,2,1,0:T(8,128)(2,1)} %param.14) | copy-start | bytes 786436
  2.3 0.9 %copy-start.1 = (f32[2,32,8,128]{3,2,1,0:T(8,128)S(1)}, f32[2,32,8,128]{3,2,1,0:T(8,128)}, u32[]{:S(2)}) copy-start(f32[2,32,8,128]{3,2,1,0:T(8,128)} %constant.11.clone.screen_ref) | copy-start | bytes 786436
  3.2 0.9 %copy-start.2 = (bf16[512,256]{1,0:T(8,128)(2,1)S(1)}, bf16[512,256]{1,0:T(8,128)(2,1)}, u32[]{:S(2)}) copy-start(bf16[512,256]{1,0:T(8,128)(2,1)} %constant.9.clone.line_ref) | copy-start | bytes 786436
  4.2 0.9 %copy-start.3 = (bf16[272,64]{1,0:T(8,128)(2,1)S(1)}, bf16[272,64]{1,0:T(8,128)(2,1)}, u32[]{:S(2)}) copy-start(bf16[272,64]{1,0:T(8,128)(2,1)} %constant.8.clone.tap_ref) | copy-start | bytes 104452
  5.1 0.8 %copy-start.4 = (f32[72,128]{1,0:T(8,128)S(1)}, f32[72,128]{1,0:T(8,128)}, u32[]{:S(2)}) copy-start(f32[72,128]{1,0:T(8,128)} %constant.10.clone.twist_ref) | copy-start | bytes 110596
  5.8 0.7 %copy-start.6 = (bf16[1,1,2048]{2,1,0:T(2,128)(2,1)S(1)}, bf16[1,1,2048]{2,1,0:T(2,128)(2,1)}, u32[]{:S(2)}) copy-start(bf16[1,1,2048]{2,1,0:T(2,128)(2,1)} %param.13) | copy-start | bytes 12292
  6.5 0.7 %copy-start.7 = (s32[1,1,2048]{2,1,0:T(1,128)S(1)}, s32[1,1,2048]{2,1,0:T(1,128)}, u32[]{:S(2)}) copy-start(s32[1,1,2048]{2,1,0:T(1,128)} %param.15) | copy-start | bytes 24580
  7.2 0.7 %copy-start.8 = (s32[1,1,2048]{2,1,0:T(1,128)S(1)}, s32[1,1,2048]{2,1,0:T(1,128)}, u32[]{:S(2)}) copy-start(s32[1,1,2048]{2,1,0:T(1,128)} %param.16) | copy-start | bytes 24580
  7.9 0.7 %copy-start.9 = (s32[1,1,2048]{2,1,0:T(1,128)S(1)}, s32[1,1,2048]{2,1,0:T(1,128)}, u32[]{:S(2)}) copy-start(s32[1,1,2048]{2,1,0:T(1,128)} %param.17) | copy-start | bytes 24580

commit v5 on v4

--- a/solution.py
+++ b/solution.py
@@ -126,8 +126,26 @@
     return [cadd(e, o) for e, o in zip(even, odd)] + [csub(e, o) for e, o in zip(even, odd)]
 
 
-def image_kernel(
-    count_ref, offset_ref, vis_ref, weight_ref, kernel_ref, tile_ref, plane_ref, chan_ref,
+def image_kernel(*refs):
+    (
+        count_ref, offset_ref, vis_ref, weight_ref, kernel_ref, tile_ref, plane_ref, chan_ref,
+        tap_ref, line_ref, twist_ref, screen_ref,
+    ) = refs[13:25]
+    fetches = [pltpu.make_async_copy(refs[i], refs[13 + i], refs[-1].at[i]) for i in range(12)]
+    for i in FETCH_ORDER:
+        fetches[i].start()
+    out_ref = refs[12]
+    image_body(
+        fetches, count_ref, offset_ref, vis_ref, weight_ref, kernel_ref, tile_ref, plane_ref, chan_ref,
+        tap_ref, line_ref, twist_ref, screen_ref, out_ref, *refs[25:-1]
+    )
+
+
+FETCH_ORDER = (8, 4, 0, 1, 2, 3, 5, 6, 7, 9, 10, 11)
+
+
+def image_body(
+    fetches, count_ref, offset_ref, vis_ref, weight_ref, kernel_ref, tile_ref, plane_ref, chan_ref,
     tap_ref, line_ref, twist_ref, screen_ref, out_ref, taps, updates, bank_of, lane_hot, grid, lines, screens, image,
     own, pair_in, pair_sum, plane_in, plane_sum, line_in, moment_own, moment_in, moment_pair,
     pair_send, pair_recv, moment_sem, plane_send, plane_recv, line_send, line_recv,
@@ -144,7 +162,11 @@
         there = (deep + j) % 8
         signal(device_id={"bl_2": there % 4, "chan_0": there // 4})
 
+    for i in (8, 4):
+        fetches[i].wait()
     taps[...] = jnp.dot(tap_ref[...], kernel_ref[...], preferred_element_type=f32)
+    for i in (0, 1, 2, 3, 5, 6, 7):
+        fetches[i].wait()
     count = jnp.broadcast_to(count_ref[0:1, 0:1], (1, CHUNK))
     offsets = [jnp.broadcast_to(offset_ref[0:1, c:c + 1], (1, CHUNK)) for c in range(16)]
 
@@ -217,6 +239,8 @@
         moment_row = jnp.where(lane == m, jnp.broadcast_to(total, (STRIP, LANES)), moment_row)
     moment_own[...] = moment_row
 
+    for i in (9, 10, 11):
+        fetches[i].wait()
     for step in range(CELLS // CHUNK):
         banks = bank_of[...]
         halves = [
@@ -381,12 +405,16 @@
 def device_image(counts, offsets, vis, weight, kernel, tile, plane, chan):
     vmem = pl.BlockSpec(memory_space=pltpu.VMEM)
     dma = pltpu.SemaphoreType.DMA
+    operands = (
+        counts, offsets, vis, weight, kernel, tile, plane, chan,
+        jnp.asarray(tap_table()), jnp.asarray(line_table()), jnp.asarray(twist_table()), jnp.asarray(screen_table()),
+    )
     return pl.pallas_call(
         image_kernel,
         out_shape=jax.ShapeDtypeStruct((2, TAYLOR, LANES), f32),
-        in_specs=[vmem] * 12,
+        in_specs=[pl.BlockSpec(memory_space=pltpu.HBM)] * 12,
         out_specs=vmem,
-        scratch_shapes=[
+        scratch_shapes=[pltpu.VMEM(a.shape, a.dtype) for a in operands] + [
             pltpu.VMEM((272, SLOTS), f32),
             pltpu.VMEM((2 * ROWS, SLOTS), bf16),
             pltpu.VMEM((SLOTS, LANES), bf16),
@@ -404,16 +432,13 @@
             pltpu.VMEM((8, LANES), f32),
             pltpu.VMEM((8, LANES), f32),
             pltpu.VMEM((8, LANES), f32),
-            dma((3,)), dma((3,)), dma((2,)), dma((4,)), dma((4,)), dma, dma,
+            dma((3,)), dma((3,)), dma((2,)), dma((4,)), dma((4,)), dma, dma, dma((12,)),
         ],
         compiler_params=pltpu.CompilerParams(
-            vmem_limit_bytes=40 * 1024 * 1024, collective_id=0, has_side_effects=True
+            vmem_limit_bytes=56 * 1024 * 1024, collective_id=0, has_side_effects=True
         ),
         name="strip_image",
-    )(
-        counts, offsets, vis, weight, kernel, tile, plane, chan,
-        jnp.asarray(tap_table()), jnp.asarray(line_table()), jnp.asarray(twist_table()), jnp.asarray(screen_table()),
-    )
+    )(*operands)
 
 
 def solve_taylor(moments, images):

time: 40.8 us -> 35 us (0.86)
  local copies, waits for them, and re-layouts: 7.93 us -> 0 us
  Pallas kernels: 31.1 us -> 32.9 us
  other arithmetic: 0.59 us -> 1.27 us
    unnamed x22 -> x0, local copies, waits for them, and re-layouts: 7.93 us -> none
    pallas_call x1, Pallas kernels: 31.1 us -> 32.9 us  [device_image(): pl.pallas_call(image_kernel, out_shape=jax.ShapeDtypeStruct((2, TAYLOR, L...]
    div x1, other arithmetic: 0.59 us -> 1.27 us  [body(): return scaled[0] / scaled[1]]
where the time goes in v5:
time: 35 us; the launch traced here: 34.9 us
  Pallas kernels  32.9 us (94%)
  other arithmetic  1.27 us (4%)
  between operations  0.66 us (2%)
    pallas_call x1, Pallas kernels, device_image(): pl.pallas_call(image_kernel, out_shape=jax.ShapeDtypeStruct((2, TAYLOR, L...  32.9 us
    div x1, other arithmetic, body(): return scaled[0] / scaled[1]  1.27 us

profile of v5, /device:TPU:1, one launch (start us, length us, event | category | flops | bytes accessed | tf_op | source)
XLA Modules:
  0.0 34.9 jit_solution(9212949269715078664)
XLA Ops:
  0.7 32.9 %strip_image.1 = f32[2,3,128]{2,1,0:T(4,128)} custom-call(s32[1,1]{1,0:T(1,128)S(6)} %copy.13.refs_0_, f32[1,16]{1,0:T(1,128)} %refs_1_.1, bf16[2,2048]{1,0:T(2,128)(2,1)} %bitcast.9, bf16[1,2048]{1,0:T(2,128)(2,1)} %bitcast.10, bf16[64,2048]{1,0:T(8,128)(2,1)} %bitcast.8, s32[1,2048]{1,0:T(1,128)} %bitcast.11, s32[1,2048]{1,0:T(1,128)} %bitcast.12, ...), custom_call_target="tpu_custom_call" | custom-call | tf_op jit(solution)/shard_map/strip_image/pallas_call | solution.py:412
  33.6 1.3 %fusion = f32[3,128]{1,0:T(4,128)} fusion(f32[2,3,128]{2,1,0:T(4,128)} %strip_image.1), kind=kLoop, calls=%fused_computation.1 | loop fusion | flops 384 | bytes 4608 | tf_op jit(solution)/shard_map/div | solution.py:468

commit v6 on v5

--- a/solution.py
+++ b/solution.py
@@ -19,6 +19,7 @@
 HALF_PLANES = 4
 WIDE = TILE + 1
 ROWS = TAYLOR * WIDE * 2 * STRIP
+SPAN = WIDE * 2 * STRIP
 CELLS = HALF_PLANES * NPIX // TILE
 BLOCKS = 32
 LANES = 128
@@ -141,22 +142,27 @@
     )
 
 
+SEND_ORDER = (10, 26, 8, 24, 2, 18, 9, 25, 11, 27, 6, 22, 14, 30, 5, 21, 7, 23, 13, 29, 15, 31, 4, 20, 12, 28, 1, 17, 3, 19, 16)
+
+
+def plane_peer(me, j):
+    there = (me + j) % 32
+    return there, {"chan_1": there // 16, "bl_0": there // 4 % 4, "bl_1": there % 4}
+
+
 FETCH_ORDER = (8, 4, 0, 1, 2, 3, 5, 6, 7, 9, 10, 11)
 
 
 def image_body(
     fetches, count_ref, offset_ref, vis_ref, weight_ref, kernel_ref, tile_ref, plane_ref, chan_ref,
     tap_ref, line_ref, twist_ref, screen_ref, out_ref, taps, updates, bank_of, lane_hot, grid, lines, screens, image,
-    own, pair_in, pair_sum, plane_in, plane_sum, line_in, moment_own, moment_in, moment_pair,
-    pair_send, pair_recv, moment_sem, plane_send, plane_recv, line_send, line_recv,
+    own, plane_in, plane_sum, line_in, moment_own, plane_send, plane_recv, line_send, line_recv,
 ):
     barrier = pltpu.get_barrier_semaphore()
     signal = functools.partial(pl.semaphore_signal, barrier, inc=1, device_id_type=MESH_ID)
-    signal(device_id={"chan_1": 1 - lax.axis_index("chan_1")})
-    flat = lax.axis_index("bl_0") * 4 + lax.axis_index("bl_1")
-    for j in range(1, 16):
-        there = (flat + j) % 16
-        signal(device_id={"bl_0": there // 4, "bl_1": there % 4})
+    me = lax.axis_index("chan_1") * 16 + lax.axis_index("bl_0") * 4 + lax.axis_index("bl_1")
+    for j in range(1, 32):
+        signal(device_id=plane_peer(me, j)[1])
     deep = lax.axis_index("chan_0") * 4 + lax.axis_index("bl_2")
     for j in range(1, 8):
         there = (deep + j) % 8
@@ -224,9 +230,9 @@
                     both = both * jnp.concatenate([coord_rows, coord_rows], axis=0)
                 high = both.astype(bf16)
                 low = (both - high.astype(f32)).astype(bf16)
-                first = (k * WIDE + e) * 16
+                first = 2 * k * SPAN + e * 16
                 updates[first:first + 16, at] = high
-                updates[ROWS + first:ROWS + first + 16, at] = low
+                updates[first + SPAN:first + SPAN + 16, at] = low
         return tuple(new_sums)
 
     sums = lax.fori_loop(
@@ -239,17 +245,20 @@
         moment_row = jnp.where(lane == m, jnp.broadcast_to(total, (STRIP, LANES)), moment_row)
     moment_own[...] = moment_row
 
+    def spread(k):
+        for step in range(CELLS // CHUNK):
+            banks = bank_of[...]
+            halves = [
+                jnp.where(banks == jnp.asarray(step * 2 + half, bf16), lane_hot[...], jnp.zeros((), bf16))
+                for half in range(CHUNK // LANES)
+            ]
+            both = jnp.dot(
+                updates[2 * SPAN * k:2 * SPAN * (k + 1)], jnp.concatenate(halves, axis=1), preferred_element_type=f32
+            )
+            grid[SPAN * k:SPAN * (k + 1), step * CHUNK:(step + 1) * CHUNK] = both[:SPAN] + both[SPAN:]
+
     for i in (9, 10, 11):
         fetches[i].wait()
-    for step in range(CELLS // CHUNK):
-        banks = bank_of[...]
-        halves = [
-            jnp.where(banks == jnp.asarray(step * 2 + half, bf16), lane_hot[...], jnp.zeros((), bf16))
-            for half in range(CHUNK // LANES)
-        ]
-        both = jnp.dot(updates[...], jnp.concatenate(halves, axis=1), preferred_element_type=f32)
-        grid[:, step * CHUNK:(step + 1) * CHUNK] = both[:ROWS] + both[ROWS:]
-
     for b in range(BLOCKS):
         one = (screen_ref[0, b], screen_ref[1, b])
         two = cmul(one, one)
@@ -307,11 +316,14 @@
                     if q < HALF_PLANES - 1:
                         image[b] = image[b] + add if q > 0 else add
                     else:
-                        own[k, pl.ds(b, STRIP, stride=BLOCKS), :] = image[b] + add
+                        total = image[b] + add
+                        first = b // 4 * 8 + b % 4
+                        own[k, pl.ds(first, 4, stride=64), :] = total[0:4]
+                        own[k, pl.ds(first + 4, 4, stride=64), :] = total[4:8]
 
     low_z = lax.axis_index("chan_0")
     core = lax.axis_index("chan_1")
-    flat = lax.axis_index("bl_0") * 4 + lax.axis_index("bl_1")
+    me = core * 16 + lax.axis_index("bl_0") * 4 + lax.axis_index("bl_1")
     deep = low_z * 4 + lax.axis_index("bl_2")
 
     def together(source, target, send, recv):
@@ -320,66 +332,26 @@
             device_id={"chan_1": 1 - core}, device_id_type=MESH_ID,
         )
 
-    def pair_copies(k):
-        return [
+    def send_plane(k):
+        for j in SEND_ORDER:
+            there, where = plane_peer(me, j)
             pltpu.make_async_remote_copy(
-                src_ref=own.at[k, pl.ds(pl.multiple_of(z * 128 + (1 - core) * 64, 64), 64)],
-                dst_ref=pair_in.at[k, pl.ds(z * 64, 64)],
-                send_sem=pair_send.at[k], recv_sem=pair_recv.at[k],
-                device_id={"chan_1": 1 - core}, device_id_type=MESH_ID,
-            )
-            for z in range(2)
-        ]
-
-    def moment_copy():
-        return pltpu.make_async_remote_copy(
-            src_ref=moment_own, dst_ref=moment_in, send_sem=moment_sem.at[0], recv_sem=moment_sem.at[1],
-            device_id={"chan_1": 1 - core}, device_id_type=MESH_ID,
-        )
-
-    def plane_copies(k):
-        copies = []
-        for j in range(1, 16):
-            there = (flat + j) % 16
-            copies.append(
-                pltpu.make_async_remote_copy(
-                    src_ref=pair_sum.at[k, there] if k < TAYLOR else moment_pair,
-                    dst_ref=plane_in.at[k, j], send_sem=plane_send.at[k], recv_sem=plane_recv.at[k],
-                    device_id={"bl_0": there // 4, "bl_1": there % 4}, device_id_type=MESH_ID,
-                )
-            )
-        return copies
-
-    def join_pair(k):
-        together(own.at[k, 0:128], pair_in.at[k], pair_send.at[k], pair_recv.at[k]).wait()
-        sums = [
-            own[k, pl.ds(pl.multiple_of(z * 128 + core * 64, 64), 64)] + pair_in[k, z * 64:z * 64 + 64] for z in range(2)
-        ]
-        for xy in range(16):
-            pair_sum[k, xy] = jnp.concatenate([sums[z][xy * 4:xy * 4 + 4] for z in range(2)], axis=0)
-        for copy in plane_copies(k):
-            copy.start()
-
+                src_ref=own.at[k, pl.ds(pl.multiple_of(there * 8, 8), 8)] if k < TAYLOR else moment_own,
+                dst_ref=plane_in.at[k, j], send_sem=plane_send.at[k], recv_sem=plane_recv.at[k],
+                device_id=where, device_id_type=MESH_ID,
+            ).start()
+
+    pl.semaphore_wait(barrier, 38)
+    send_plane(TAYLOR)
     for k in range(TAYLOR):
+        spread(k)
         one_term(k)
-        if k == 0:
-            pl.semaphore_wait(barrier, 23)
-            moment_copy().start()
-        for copy in pair_copies(k):
-            copy.start()
-        if k == 0:
-            moment_copy().wait()
-            moment_pair[...] = moment_own[...] + moment_in[...]
-            for copy in plane_copies(TAYLOR):
-                copy.start()
-        else:
-            join_pair(k - 1)
-    join_pair(TAYLOR - 1)
+        send_plane(k)
 
     for k in (TAYLOR, 0, 1, 2):
-        total = pair_sum[k, flat] if k < TAYLOR else moment_pair[...]
-        together(pair_sum.at[0, 0:15], plane_in.at[k, 1:16], plane_send.at[k], plane_recv.at[k]).wait()
-        for j in range(1, 16):
+        total = own[k, pl.ds(pl.multiple_of(me * 8, 8), 8)] if k < TAYLOR else moment_own[...]
+        together(plane_in.at[3, 1:32], plane_in.at[k, 1:32], plane_send.at[k], plane_recv.at[k]).wait()
+        for j in range(1, 32):
             total = total + plane_in[k, j]
         for r in range(8):
             plane_sum[r, k:k + 1] = total[r:r + 1]
@@ -424,15 +396,11 @@
             pltpu.VMEM((HALF_PLANES, 2, BLOCKS, STRIP, LANES), f32),
             pltpu.VMEM((BLOCKS, STRIP, LANES), f32),
             pltpu.VMEM((TAYLOR, 256, LANES), f32),
-            pltpu.VMEM((TAYLOR, 128, LANES), f32),
-            pltpu.VMEM((TAYLOR, 16, 8, LANES), f32),
-            pltpu.VMEM((TAYLOR + 1, 16, 8, LANES), f32),
+            pltpu.VMEM((TAYLOR + 1, 32, 8, LANES), f32),
             pltpu.VMEM((8, 4, LANES), f32),
             pltpu.VMEM((8, 4, LANES), f32),
             pltpu.VMEM((8, LANES), f32),
-            pltpu.VMEM((8, LANES), f32),
-            pltpu.VMEM((8, LANES), f32),
-            dma((3,)), dma((3,)), dma((2,)), dma((4,)), dma((4,)), dma, dma, dma((12,)),
+            dma((4,)), dma((4,)), dma, dma, dma((12,)),
         ],
         compiler_params=pltpu.CompilerParams(
             vmem_limit_bytes=56 * 1024 * 1024, collective_id=0, has_side_effects=True

time: 35 us -> 34.2 us (0.977)
  Pallas kernels: 32.9 us -> 32.2 us
    pallas_call x1, Pallas kernels: 32.9 us -> 32.2 us  [device_image(): pl.pallas_call(image_kernel, out_shape=jax.ShapeDtypeStruct((2, TAYLOR, L...]
where the time goes in v6:
time: 34.2 us; the launch traced here: 34.1 us
  Pallas kernels  32.2 us (94%)
  other arithmetic  1.27 us (4%)
  between operations  0.66 us (2%)
    pallas_call x1, Pallas kernels, device_image(): pl.pallas_call(image_kernel, out_shape=jax.ShapeDtypeStruct((2, TAYLOR, L...  32.2 us
    div x1, other arithmetic, body(): return scaled[0] / scaled[1]  1.27 us

profile of v6, /device:TPU:1, one launch (start us, length us, event | category | flops | bytes accessed | tf_op | source)
XLA Modules:
  0.0 34.1 jit_solution(4072650772125749380)
XLA Ops:
  0.7 32.2 %strip_image.1 = f32[2,3,128]{2,1,0:T(4,128)} custom-call(s32[1,1]{1,0:T(1,128)S(6)} %copy.13.refs_0_, f32[1,16]{1,0:T(1,128)} %refs_1_.1, bf16[2,2048]{1,0:T(2,128)(2,1)} %bitcast.9, bf16[1,2048]{1,0:T(2,128)(2,1)} %bitcast.10, bf16[64,2048]{1,0:T(8,128)(2,1)} %bitcast.8, s32[1,2048]{1,0:T(1,128)} %bitcast.11, s32[1,2048]{1,0:T(1,128)} %bitcast.12, ...), custom_call_target="tpu_custom_call" | custom-call | tf_op jit(solution)/shard_map/strip_image/pallas_call | solution.py:384
  32.8 1.3 %fusion = f32[3,128]{1,0:T(4,128)} fusion(f32[2,3,128]{2,1,0:T(4,128)} %strip_image.1), kind=kLoop, calls=%fused_computation.1 | loop fusion | flops 384 | bytes 4608 | tf_op jit(solution)/shard_map/div | solution.py:436

commit v7 on v6

--- a/solution.py
+++ b/solution.py
@@ -46,9 +46,9 @@
         table[0, e, :, :, e] = np.cos(angle)
         table[1, e, :, :, e] = np.sin(angle)
     high, low = split_pair(table.reshape(2 * TILE * STRIP, TILE * TILE))
-    ones = np.zeros((16, TILE * TILE), np.float32)
-    ones[0] = 1.0
-    return np.concatenate([high, low, ones.astype(bf16)], axis=0)
+    ones = np.zeros((16, 2 * TILE * TILE), np.float32)
+    ones[0, :TILE * TILE] = 1.0
+    return np.concatenate([np.concatenate([high, low], axis=1), ones.astype(bf16)], axis=0)
 
 
 def line_table():
@@ -128,21 +128,25 @@
 
 
 def image_kernel(*refs):
+    offset_ref = refs[0]
     (
-        count_ref, offset_ref, vis_ref, weight_ref, kernel_ref, tile_ref, plane_ref, chan_ref,
+        count_ref, vis_ref, weight_ref, kernel_ref, tile_ref, plane_ref, chan_ref,
         tap_ref, line_ref, twist_ref, screen_ref,
-    ) = refs[13:25]
-    fetches = [pltpu.make_async_copy(refs[i], refs[13 + i], refs[-1].at[i]) for i in range(12)]
+    ) = refs[13:24]
+    fetches = [pltpu.make_async_copy(refs[1 + i], refs[13 + i], refs[-1].at[i]) for i in range(11)]
     for i in FETCH_ORDER:
         fetches[i].start()
     out_ref = refs[12]
     image_body(
         fetches, count_ref, offset_ref, vis_ref, weight_ref, kernel_ref, tile_ref, plane_ref, chan_ref,
-        tap_ref, line_ref, twist_ref, screen_ref, out_ref, *refs[25:-1]
-    )
-
-
-SEND_ORDER = (10, 26, 8, 24, 2, 18, 9, 25, 11, 27, 6, 22, 14, 30, 5, 21, 7, 23, 13, 29, 15, 31, 4, 20, 12, 28, 1, 17, 3, 19, 16)
+        tap_ref, line_ref, twist_ref, screen_ref, out_ref, *refs[24:-1]
+    )
+
+
+START_X = (0.0, 0.8, 1.7, 1.8)
+START_Z = (0, 1, 2, 3, 7, 4, 5, 6)
+PLANE_ORDER = sorted(range(32), key=lambda t: START_X[t // 4 % 4] + START_X[t % 4] + 1.2 * (t // 16))
+LINE_ORDER = tuple(z % 2 * 4 + z // 2 for z in START_Z)
 
 
 def plane_peer(me, j):
@@ -150,7 +154,7 @@
     return there, {"chan_1": there // 16, "bl_0": there // 4 % 4, "bl_1": there % 4}
 
 
-FETCH_ORDER = (8, 4, 0, 1, 2, 3, 5, 6, 7, 9, 10, 11)
+FETCH_ORDER = (7, 3, 0, 1, 2, 4, 5, 6, 8, 9, 10)
 
 
 def image_body(
@@ -168,10 +172,12 @@
         there = (deep + j) % 8
         signal(device_id={"bl_2": there % 4, "chan_0": there // 4})
 
-    for i in (8, 4):
+    for i in (7, 3):
         fetches[i].wait()
-    taps[...] = jnp.dot(tap_ref[...], kernel_ref[...], preferred_element_type=f32)
-    for i in (0, 1, 2, 3, 5, 6, 7):
+    taps[...] = jnp.dot(
+        tap_ref[...], jnp.concatenate([kernel_ref[...], kernel_ref[...]], axis=0), preferred_element_type=f32
+    )
+    for i in (0, 1, 2, 4, 5, 6):
         fetches[i].wait()
     count = jnp.broadcast_to(count_ref[0:1, 0:1], (1, CHUNK))
     offsets = [jnp.broadcast_to(offset_ref[0:1, c:c + 1], (1, CHUNK)) for c in range(16)]
@@ -194,7 +200,7 @@
         bank_of[at, :] = across(half * 4 + (tile_v & 3)).astype(bf16)
         lane = lax.broadcasted_iota(jnp.int32, (CHUNK, LANES), 1).astype(f32)
         lane_hot[at, :] = jnp.where(across(tile_v >> 2) == lane, 1.0, 0.0).astype(bf16)
-        weighted = weight * taps[256:257, at]
+        weighted = weight * taps[128:129, at]
         new_sums = []
         power = weighted
         for m in range(MOMENTS):
@@ -213,8 +219,7 @@
         for e in range(TILE):
             r = slice(e * STRIP, (e + 1) * STRIP)
             i = slice(64 + e * STRIP, 64 + (e + 1) * STRIP)
-            tap_r = taps[r, at] + taps[128 + r.start:128 + r.stop, at]
-            tap_i = taps[i, at] + taps[128 + i.start:128 + i.stop, at]
+            tap_r, tap_i = taps[r, at], taps[i, at]
             parts.append(
                 (turned[0] * tap_r - turned[1] * tap_i, flipped[0] * tap_i + flipped[1] * tap_r)
             )
@@ -257,7 +262,7 @@
             )
             grid[SPAN * k:SPAN * (k + 1), step * CHUNK:(step + 1) * CHUNK] = both[:SPAN] + both[SPAN:]
 
-    for i in (9, 10, 11):
+    for i in (8, 9, 10):
         fetches[i].wait()
     for b in range(BLOCKS):
         one = (screen_ref[0, b], screen_ref[1, b])
@@ -333,19 +338,20 @@
         )
 
     def send_plane(k):
-        for j in SEND_ORDER:
-            there, where = plane_peer(me, j)
-            pltpu.make_async_remote_copy(
-                src_ref=own.at[k, pl.ds(pl.multiple_of(there * 8, 8), 8)] if k < TAYLOR else moment_own,
-                dst_ref=plane_in.at[k, j], send_sem=plane_send.at[k], recv_sem=plane_recv.at[k],
-                device_id=where, device_id_type=MESH_ID,
-            ).start()
-
-    pl.semaphore_wait(barrier, 38)
-    send_plane(TAYLOR)
+        for there in PLANE_ORDER:
+            copy = pltpu.make_async_remote_copy(
+                src_ref=own.at[k, there * 8:there * 8 + 8] if k < TAYLOR else moment_own,
+                dst_ref=plane_in.at[k, (me - there) % 32], send_sem=plane_send.at[k], recv_sem=plane_recv.at[k],
+                device_id={"chan_1": there // 16, "bl_0": there // 4 % 4, "bl_1": there % 4}, device_id_type=MESH_ID,
+            )
+            pl.when(me != there)(copy.start)
+
     for k in range(TAYLOR):
         spread(k)
         one_term(k)
+        if k == 0:
+            pl.semaphore_wait(barrier, 38)
+            send_plane(TAYLOR)
         send_plane(k)
 
     for k in (TAYLOR, 0, 1, 2):
@@ -356,12 +362,12 @@
         for r in range(8):
             plane_sum[r, k:k + 1] = total[r:r + 1]
 
-    for j in range(1, 8):
-        there = (deep + j) % 8
-        pltpu.make_async_remote_copy(
-            src_ref=plane_sum.at[there], dst_ref=line_in.at[j], send_sem=line_send, recv_sem=line_recv,
+    for there in LINE_ORDER:
+        copy = pltpu.make_async_remote_copy(
+            src_ref=plane_sum.at[there], dst_ref=line_in.at[(deep - there) % 8], send_sem=line_send, recv_sem=line_recv,
             device_id={"bl_2": there % 4, "chan_0": there // 4}, device_id_type=MESH_ID,
-        ).start()
+        )
+        pl.when(deep != there)(copy.start)
     total = plane_sum[deep]
     together(plane_sum.at[0:7], line_in.at[1:8], line_send, line_recv).wait()
     for j in range(1, 8):
@@ -378,16 +384,16 @@
     vmem = pl.BlockSpec(memory_space=pltpu.VMEM)
     dma = pltpu.SemaphoreType.DMA
     operands = (
-        counts, offsets, vis, weight, kernel, tile, plane, chan,
+        counts, vis, weight, kernel, tile, plane, chan,
         jnp.asarray(tap_table()), jnp.asarray(line_table()), jnp.asarray(twist_table()), jnp.asarray(screen_table()),
     )
     return pl.pallas_call(
         image_kernel,
         out_shape=jax.ShapeDtypeStruct((2, TAYLOR, LANES), f32),
-        in_specs=[pl.BlockSpec(memory_space=pltpu.HBM)] * 12,
+        in_specs=[vmem] + [pl.BlockSpec(memory_space=pltpu.HBM)] * 11,
         out_specs=vmem,
         scratch_shapes=[pltpu.VMEM(a.shape, a.dtype) for a in operands] + [
-            pltpu.VMEM((272, SLOTS), f32),
+            pltpu.VMEM((144, SLOTS), f32),
             pltpu.VMEM((2 * ROWS, SLOTS), bf16),
             pltpu.VMEM((SLOTS, LANES), bf16),
             pltpu.VMEM((SLOTS, LANES), bf16),
@@ -400,13 +406,13 @@
             pltpu.VMEM((8, 4, LANES), f32),
             pltpu.VMEM((8, 4, LANES), f32),
             pltpu.VMEM((8, LANES), f32),
-            dma((4,)), dma((4,)), dma, dma, dma((12,)),
+            dma((4,)), dma((4,)), dma, dma, dma((11,)),
         ],
         compiler_params=pltpu.CompilerParams(
-            vmem_limit_bytes=56 * 1024 * 1024, collective_id=0, has_side_effects=True
+            vmem_limit_bytes=55220 * 1024, collective_id=0, has_side_effects=True
         ),
         name="strip_image",
-    )(*operands)
+    )(offsets, *operands)
 
 
 def solve_taylor(moments, images):

time: 34.2 us -> 33.2 us (0.971)
  Pallas kernels: 32.2 us -> 31.2 us
  other arithmetic: 1.27 us -> 0.59 us
  local copies, waits for them, and re-layouts: 0 us -> 0.65 us
    pallas_call x1, Pallas kernels: 32.2 us -> 31.2 us  [device_image(): pl.pallas_call(image_kernel, out_shape=jax.ShapeDtypeStruct((2, TAYLOR, L...]
    div x1, other arithmetic: 1.27 us -> 0.59 us  [body(): return scaled[0] / scaled[1]]
    unnamed x0 -> x2, local copies, waits for them, and re-layouts: none -> 0.65 us
where the time goes in v7:
time: 33.2 us; the launch traced here: 33.1 us
  Pallas kernels  31.2 us (94%)
  between operations  0.67 us (2%)
  local copies, waits for them, and re-layouts  0.65 us (2%)
  other arithmetic  0.59 us (2%)
    pallas_call x1, Pallas kernels, device_image(): pl.pallas_call(image_kernel, out_shape=jax.ShapeDtypeStruct((2, TAYLOR, L...  31.2 us

profile of v7, /device:TPU:1, one launch (start us, length us, event | category | flops | bytes accessed | tf_op | source)
XLA Modules:
  0.0 33.1 jit_solution(2207686004191494769)
XLA Ops:
  0.7 0.0 copy-start
  0.7 0.6 %copy-done = f32[1,16]{1,0:T(1,128)S(1)} copy-done((f32[1,16]{1,0:T(1,128)S(1)}, f32[1,16]{1,0:T(1,128)}, u32[]{:S(2)}) %copy-start) | copy-done | bytes 88
  1.3 31.2 %strip_image.1 = f32[2,3,128]{2,1,0:T(4,128)S(1)} custom-call(f32[1,16]{1,0:T(1,128)S(1)} %copy-done, s32[1,1]{1,0:T(1,128)S(6)} %copy.13.refs_1_, bf16[2,2048]{1,0:T(2,128)(2,1)} %bitcast.9, bf16[1,2048]{1,0:T(2,128)(2,1)} %bitcast.10, bf16[64,2048]{1,0:T(8,128)(2,1)} %bitcast.8, s32[1,2048]{1,0:T(1,128)} %bitcast.11, s32[1,2048]{1,0:T(1,128)} %bitcast.12, ...), custom_call_target="tpu_custom_call" | custom-call | tf_op jit(solution)/shard_map/strip_image/pallas_call | solution.py:390
  32.5 0.6 %fusion = f32[3,128]{1,0:T(4,128)} fusion(f32[2,3,128]{2,1,0:T(4,128)S(1)} %strip_image.1), kind=kLoop, calls=%fused_computation.1 | loop fusion | flops 384 | bytes 4608 | tf_op jit(solution)/shard_map/div | solution.py:442
Async XLA Ops:
  0.7 0.7 %copy-start = (f32[1,16]{1,0:T(1,128)S(1)}, f32[1,16]{1,0:T(1,128)}, u32[]{:S(2)}) copy-start(f32[1,16]{1,0:T(1,128)} %refs_0_.1) | copy-start | bytes 196

commit v8 on v7

--- a/solution.py
+++ b/solution.py
@@ -159,7 +159,7 @@
 
 def image_body(
     fetches, count_ref, offset_ref, vis_ref, weight_ref, kernel_ref, tile_ref, plane_ref, chan_ref,
-    tap_ref, line_ref, twist_ref, screen_ref, out_ref, taps, updates, bank_of, lane_hot, grid, lines, screens, image,
+    tap_ref, line_ref, twist_ref, screen_ref, out_ref, updates, bank_of, lane_hot, grid, lines, screens, image,
     own, plane_in, plane_sum, line_in, moment_own, plane_send, plane_recv, line_send, line_recv,
 ):
     barrier = pltpu.get_barrier_semaphore()
@@ -174,9 +174,6 @@
 
     for i in (7, 3):
         fetches[i].wait()
-    taps[...] = jnp.dot(
-        tap_ref[...], jnp.concatenate([kernel_ref[...], kernel_ref[...]], axis=0), preferred_element_type=f32
-    )
     for i in (0, 1, 2, 4, 5, 6):
         fetches[i].wait()
     count = jnp.broadcast_to(count_ref[0:1, 0:1], (1, CHUNK))
@@ -184,6 +181,8 @@
 
     def one_chunk(step, sums):
         at = pl.ds(pl.multiple_of(step * CHUNK, CHUNK), CHUNK)
+        chunk_kernel = kernel_ref[:, at]
+        taps = jnp.dot(tap_ref[...], jnp.concatenate([chunk_kernel, chunk_kernel], axis=0), preferred_element_type=f32)
         slot = step * CHUNK + lax.broadcasted_iota(jnp.int32, (1, CHUNK), 1)
         weight = jnp.where(slot < count, weight_ref[:, at].astype(f32), 0.0)
         chan = chan_ref[:, at]
@@ -200,7 +199,7 @@
         bank_of[at, :] = across(half * 4 + (tile_v & 3)).astype(bf16)
         lane = lax.broadcasted_iota(jnp.int32, (CHUNK, LANES), 1).astype(f32)
         lane_hot[at, :] = jnp.where(across(tile_v >> 2) == lane, 1.0, 0.0).astype(bf16)
-        weighted = weight * taps[128:129, at]
+        weighted = weight * taps[128:129]
         new_sums = []
         power = weighted
         for m in range(MOMENTS):
@@ -219,7 +218,7 @@
         for e in range(TILE):
             r = slice(e * STRIP, (e + 1) * STRIP)
             i = slice(64 + e * STRIP, 64 + (e + 1) * STRIP)
-            tap_r, tap_i = taps[r, at], taps[i, at]
+            tap_r, tap_i = taps[r], taps[i]
             parts.append(
                 (turned[0] * tap_r - turned[1] * tap_i, flipped[0] * tap_i + flipped[1] * tap_r)
             )
@@ -241,7 +240,8 @@
         return tuple(new_sums)
 
     sums = lax.fori_loop(
-        0, SLOTS // CHUNK, one_chunk, tuple(jnp.zeros((1, CHUNK), f32) for _ in range(MOMENTS))
+        0, SLOTS // CHUNK, one_chunk, tuple(jnp.zeros((1, CHUNK), f32) for _ in range(MOMENTS)),
+        unroll=True,
     )
     lane = lax.broadcasted_iota(jnp.int32, (STRIP, LANES), 1)
     moment_row = jnp.zeros((STRIP, LANES), f32)
@@ -393,7 +393,6 @@
         in_specs=[vmem] + [pl.BlockSpec(memory_space=pltpu.HBM)] * 11,
         out_specs=vmem,
         scratch_shapes=[pltpu.VMEM(a.shape, a.dtype) for a in operands] + [
-            pltpu.VMEM((144, SLOTS), f32),
             pltpu.VMEM((2 * ROWS, SLOTS), bf16),
             pltpu.VMEM((SLOTS, LANES), bf16),
             pltpu.VMEM((SLOTS, LANES), bf16),

time: 33.2 us -> 32.3 us (0.973)
  Pallas kernels: 31.2 us -> 30.3 us
    pallas_call x1, Pallas kernels: 31.2 us -> 30.3 us  [device_image(): pl.pallas_call(image_kernel, out_shape=jax.ShapeDtypeStruct((2, TAYLOR, L...]
where the time goes in v8:
time: 32.3 us; the launch traced here: 32.2 us
  Pallas kernels  30.3 us (94%)
  between operations  0.67 us (2%)
  local copies, waits for them, and re-layouts  0.65 us (2%)
  other arithmetic  0.59 us (2%)
    pallas_call x1, Pallas kernels, device_image(): pl.pallas_call(image_kernel, out_shape=jax.ShapeDtypeStruct((2, TAYLOR, L...  30.3 us
    unnamed x2, local copies, waits for them, and re-layouts  0.65 us

profile of v8, /device:TPU:1, one launch (start us, length us, event | category | flops | bytes accessed | tf_op | source)
XLA Modules:
  0.0 32.2 jit_solution(6246309815649261443)
XLA Ops:
  0.7 0.0 copy-start
  0.7 0.6 %copy-done = f32[1,16]{1,0:T(1,128)S(1)} copy-done((f32[1,16]{1,0:T(1,128)S(1)}, f32[1,16]{1,0:T(1,128)}, u32[]{:S(2)}) %copy-start) | copy-done | bytes 88
  1.3 30.3 %strip_image.1 = f32[2,3,128]{2,1,0:T(4,128)S(1)} custom-call(f32[1,16]{1,0:T(1,128)S(1)} %copy-done, s32[1,1]{1,0:T(1,128)S(6)} %copy.13.refs_1_, bf16[2,2048]{1,0:T(2,128)(2,1)} %bitcast.9, bf16[1,2048]{1,0:T(2,128)(2,1)} %bitcast.10, bf16[64,2048]{1,0:T(8,128)(2,1)} %bitcast.8, s32[1,2048]{1,0:T(1,128)} %bitcast.11, s32[1,2048]{1,0:T(1,128)} %bitcast.12, ...), custom_call_target="tpu_custom_call" | custom-call | tf_op jit(solution)/shard_map/strip_image/pallas_call | solution.py:390
  31.6 0.6 %fusion = f32[3,128]{1,0:T(4,128)} fusion(f32[2,3,128]{2,1,0:T(4,128)S(1)} %strip_image.1), kind=kLoop, calls=%fused_computation.1 | loop fusion | flops 384 | bytes 4608 | tf_op jit(solution)/shard_map/div | solution.py:441
Async XLA Ops:
  0.7 0.7 %copy-start = (f32[1,16]{1,0:T(1,128)S(1)}, f32[1,16]{1,0:T(1,128)}, u32[]{:S(2)}) copy-start(f32[1,16]{1,0:T(1,128)} %refs_0_.1) | copy-start | bytes 196

commit v9 on v8

--- a/solution.py
+++ b/solution.py
@@ -159,7 +159,7 @@
 
 def image_body(
     fetches, count_ref, offset_ref, vis_ref, weight_ref, kernel_ref, tile_ref, plane_ref, chan_ref,
-    tap_ref, line_ref, twist_ref, screen_ref, out_ref, updates, bank_of, lane_hot, grid, lines, screens, image,
+    tap_ref, line_ref, twist_ref, screen_ref, out_ref, updates, bank_of, lane_hot, hot, grid, lines, screens, image,
     own, plane_in, plane_sum, line_in, moment_own, plane_send, plane_recv, line_send, line_recv,
 ):
     barrier = pltpu.get_barrier_semaphore()
@@ -252,26 +252,30 @@
 
     def spread(k):
         for step in range(CELLS // CHUNK):
-            banks = bank_of[...]
-            halves = [
-                jnp.where(banks == jnp.asarray(step * 2 + half, bf16), lane_hot[...], jnp.zeros((), bf16))
-                for half in range(CHUNK // LANES)
-            ]
-            both = jnp.dot(
-                updates[2 * SPAN * k:2 * SPAN * (k + 1)], jnp.concatenate(halves, axis=1), preferred_element_type=f32
-            )
+            if k == 0:
+                banks = bank_of[...]
+                halves = [
+                    jnp.where(banks == jnp.asarray(step * 2 + half, bf16), lane_hot[...], jnp.zeros((), bf16))
+                    for half in range(CHUNK // LANES)
+                ]
+                one_hot = jnp.concatenate(halves, axis=1)
+                hot[step] = one_hot
+            else:
+                one_hot = hot[step]
+            both = jnp.dot(updates[2 * SPAN * k:2 * SPAN * (k + 1)], one_hot, preferred_element_type=f32)
             grid[SPAN * k:SPAN * (k + 1), step * CHUNK:(step + 1) * CHUNK] = both[:SPAN] + both[SPAN:]
 
-    for i in (8, 9, 10):
-        fetches[i].wait()
-    for b in range(BLOCKS):
-        one = (screen_ref[0, b], screen_ref[1, b])
-        two = cmul(one, one)
-        for q in range(HALF_PLANES):
-            screens[q, 0, b] = one[0]
-            screens[q, 1, b] = one[1]
-            if q < HALF_PLANES - 1:
-                one = cmul(one, two)
+    def tables():
+        for i in (8, 9, 10):
+            fetches[i].wait()
+        for b in range(BLOCKS):
+            one = (screen_ref[0, b], screen_ref[1, b])
+            two = cmul(one, one)
+            for q in range(HALF_PLANES):
+                screens[q, 0, b] = one[0]
+                screens[q, 1, b] = one[1]
+                if q < HALF_PLANES - 1:
+                    one = cmul(one, two)
 
     def piece(k, e, part, q, vb):
         first = ((k * WIDE + e) * 2 + part) * STRIP
@@ -348,6 +352,8 @@
 
     for k in range(TAYLOR):
         spread(k)
+        if k == 0:
+            tables()
         one_term(k)
         if k == 0:
             pl.semaphore_wait(barrier, 38)
@@ -396,6 +402,7 @@
             pltpu.VMEM((2 * ROWS, SLOTS), bf16),
             pltpu.VMEM((SLOTS, LANES), bf16),
             pltpu.VMEM((SLOTS, LANES), bf16),
+            pltpu.VMEM((CELLS // CHUNK, SLOTS, CHUNK), bf16),
             pltpu.VMEM((ROWS, CELLS), f32),
             pltpu.VMEM((HALF_PLANES, 256, 256), f32),
             pltpu.VMEM((HALF_PLANES, 2, BLOCKS, STRIP, LANES), f32),

time: 32.3 us -> 32.9 us (1.019)
  Pallas kernels: 30.3 us -> 30.9 us
    pallas_call x1, Pallas kernels: 30.3 us -> 30.9 us  [device_image(): pl.pallas_call(image_kernel, out_shape=jax.ShapeDtypeStruct((2, TAYLOR, L...]
where the time goes in v9:
time: 32.9 us; the launch traced here: 32.8 us
  Pallas kernels  30.9 us (94%)
  between operations  0.67 us (2%)
  local copies, waits for them, and re-layouts  0.65 us (2%)
  other arithmetic  0.59 us (2%)
    pallas_call x1, Pallas kernels, device_image(): pl.pallas_call(image_kernel, out_shape=jax.ShapeDtypeStruct((2, TAYLOR, L...  30.9 us

profile of v9, /device:TPU:1, one launch (start us, length us, event | category | flops | bytes accessed | tf_op | source)
XLA Modules:
  0.0 32.8 jit_solution(660627518847264419)
XLA Ops:
  0.7 0.0 copy-start
  0.7 0.6 %copy-done = f32[1,16]{1,0:T(1,128)S(1)} copy-done((f32[1,16]{1,0:T(1,128)S(1)}, f32[1,16]{1,0:T(1,128)}, u32[]{:S(2)}) %copy-start) | copy-done | bytes 88
  1.3 30.9 %strip_image.1 = f32[2,3,128]{2,1,0:T(4,128)S(1)} custom-call(f32[1,16]{1,0:T(1,128)S(1)} %copy-done, s32[1,1]{1,0:T(1,128)S(6)} %copy.13.refs_1_, bf16[2,2048]{1,0:T(2,128)(2,1)} %bitcast.9, bf16[1,2048]{1,0:T(2,128)(2,1)} %bitcast.10, bf16[64,2048]{1,0:T(8,128)(2,1)} %bitcast.8, s32[1,2048]{1,0:T(1,128)} %bitcast.11, s32[1,2048]{1,0:T(1,128)} %bitcast.12, ...), custom_call_target="tpu_custom_call" | custom-call | tf_op jit(solution)/shard_map/strip_image/pallas_call | solution.py:396
  32.2 0.6 %fusion = f32[3,128]{1,0:T(4,128)} fusion(f32[2,3,128]{2,1,0:T(4,128)S(1)} %strip_image.1), kind=kLoop, calls=%fused_computation.1 | loop fusion | flops 384 | bytes 4608 | tf_op jit(solution)/shard_map/div | solution.py:448
Async XLA Ops:
  0.7 0.7 %copy-start = (f32[1,16]{1,0:T(1,128)S(1)}, f32[1,16]{1,0:T(1,128)}, u32[]{:S(2)}) copy-start(f32[1,16]{1,0:T(1,128)} %refs_0_.1) | copy-start | bytes 196

commit v10 on v8

--- a/solution.py
+++ b/solution.py
@@ -159,7 +159,7 @@
 
 def image_body(
     fetches, count_ref, offset_ref, vis_ref, weight_ref, kernel_ref, tile_ref, plane_ref, chan_ref,
-    tap_ref, line_ref, twist_ref, screen_ref, out_ref, updates, bank_of, lane_hot, grid, lines, screens, image,
+    tap_ref, line_ref, twist_ref, screen_ref, out_ref, updates, bank_of, lane_hot, hot, grid, lines, screens, image,
     own, plane_in, plane_sum, line_in, moment_own, plane_send, plane_recv, line_send, line_recv,
 ):
     barrier = pltpu.get_barrier_semaphore()
@@ -252,14 +252,17 @@
 
     def spread(k):
         for step in range(CELLS // CHUNK):
-            banks = bank_of[...]
-            halves = [
-                jnp.where(banks == jnp.asarray(step * 2 + half, bf16), lane_hot[...], jnp.zeros((), bf16))
-                for half in range(CHUNK // LANES)
-            ]
-            both = jnp.dot(
-                updates[2 * SPAN * k:2 * SPAN * (k + 1)], jnp.concatenate(halves, axis=1), preferred_element_type=f32
-            )
+            if k == 0:
+                banks = bank_of[...]
+                halves = [
+                    jnp.where(banks == jnp.asarray(step * 2 + half, bf16), lane_hot[...], jnp.zeros((), bf16))
+                    for half in range(CHUNK // LANES)
+                ]
+                one_hot = jnp.concatenate(halves, axis=1)
+                hot[step] = one_hot
+            else:
+                one_hot = hot[step]
+            both = jnp.dot(updates[2 * SPAN * k:2 * SPAN * (k + 1)], one_hot, preferred_element_type=f32)
             grid[SPAN * k:SPAN * (k + 1), step * CHUNK:(step + 1) * CHUNK] = both[:SPAN] + both[SPAN:]
 
     for i in (8, 9, 10):
@@ -396,6 +399,7 @@
             pltpu.VMEM((2 * ROWS, SLOTS), bf16),
             pltpu.VMEM((SLOTS, LANES), bf16),
             pltpu.VMEM((SLOTS, LANES), bf16),
+            pltpu.VMEM((CELLS // CHUNK, SLOTS, CHUNK), bf16),
             pltpu.VMEM((ROWS, CELLS), f32),
             pltpu.VMEM((HALF_PLANES, 256, 256), f32),
             pltpu.VMEM((HALF_PLANES, 2, BLOCKS, STRIP, LANES), f32),

time: 32.3 us -> 32.4 us (level)
  no operation moved by 1% of the time
where the time goes in v10:
time: 32.4 us; the launch traced here: 32.3 us
  Pallas kernels  30.3 us (94%)
  between operations  0.67 us (2%)
  local copies, waits for them, and re-layouts  0.65 us (2%)
  other arithmetic  0.59 us (2%)
    pallas_call x1, Pallas kernels, device_image(): pl.pallas_call(image_kernel, out_shape=jax.ShapeDtypeStruct((2, TAYLOR, L...  30.3 us
    unnamed x2, local copies, waits for them, and re-layouts  0.65 us

profile of v10, /device:TPU:1, one launch (start us, length us, event | category | flops | bytes accessed | tf_op | source)
XLA Modules:
  0.0 32.3 jit_solution(7744674544741708622)
XLA Ops:
  0.7 0.0 copy-start
  0.7 0.6 %copy-done = f32[1,16]{1,0:T(1,128)S(1)} copy-done((f32[1,16]{1,0:T(1,128)S(1)}, f32[1,16]{1,0:T(1,128)}, u32[]{:S(2)}) %copy-start) | copy-done | bytes 88
  1.3 30.3 %strip_image.1 = f32[2,3,128]{2,1,0:T(4,128)S(1)} custom-call(f32[1,16]{1,0:T(1,128)S(1)} %copy-done, s32[1,1]{1,0:T(1,128)S(6)} %copy.13.refs_1_, bf16[2,2048]{1,0:T(2,128)(2,1)} %bitcast.9, bf16[1,2048]{1,0:T(2,128)(2,1)} %bitcast.10, bf16[64,2048]{1,0:T(8,128)(2,1)} %bitcast.8, s32[1,2048]{1,0:T(1,128)} %bitcast.11, s32[1,2048]{1,0:T(1,128)} %bitcast.12, ...), custom_call_target="tpu_custom_call" | custom-call | tf_op jit(solution)/shard_map/strip_image/pallas_call | solution.py:393
  31.7 0.6 %fusion = f32[3,128]{1,0:T(4,128)} fusion(f32[2,3,128]{2,1,0:T(4,128)S(1)} %strip_image.1), kind=kLoop, calls=%fused_computation.1 | loop fusion | flops 384 | bytes 4608 | tf_op jit(solution)/shard_map/div | solution.py:445
Async XLA Ops:
  0.7 0.7 %copy-start = (f32[1,16]{1,0:T(1,128)S(1)}, f32[1,16]{1,0:T(1,128)}, u32[]{:S(2)}) copy-start(f32[1,16]{1,0:T(1,128)} %refs_0_.1) | copy-start | bytes 196

commit v11 on v10

--- a/solution.py
+++ b/solution.py
@@ -147,6 +147,12 @@
 START_Z = (0, 1, 2, 3, 7, 4, 5, 6)
 PLANE_ORDER = sorted(range(32), key=lambda t: START_X[t // 4 % 4] + START_X[t % 4] + 1.2 * (t // 16))
 LINE_ORDER = tuple(z % 2 * 4 + z // 2 for z in START_Z)
+
+
+def tree_sum(values):
+    while len(values) > 1:
+        values = [a + b for a, b in zip(values[0::2], values[1::2])]
+    return values[0]
 
 
 def plane_peer(me, j):
@@ -360,8 +366,7 @@
     for k in (TAYLOR, 0, 1, 2):
         total = own[k, pl.ds(pl.multiple_of(me * 8, 8), 8)] if k < TAYLOR else moment_own[...]
         together(plane_in.at[3, 1:32], plane_in.at[k, 1:32], plane_send.at[k], plane_recv.at[k]).wait()
-        for j in range(1, 32):
-            total = total + plane_in[k, j]
+        total = tree_sum([total] + [plane_in[k, j] for j in range(1, 32)])
         for r in range(8):
             plane_sum[r, k:k + 1] = total[r:r + 1]
 
@@ -373,8 +378,7 @@
         pl.when(deep != there)(copy.start)
     total = plane_sum[deep]
     together(plane_sum.at[0:7], line_in.at[1:8], line_send, line_recv).wait()
-    for j in range(1, 8):
-        total = total + line_in[j]
+    total = tree_sum([total] + [line_in[j] for j in range(1, 8)])
     moments = [total[TAYLOR:TAYLOR + 1, m:m + 1] for m in range(MOMENTS)]
     images = [total[k:k + 1] for k in range(TAYLOR)]
     rows, determinant = solve_taylor(moments, images)

time: 32.4 us -> 32.3 us (level)
  no operation moved by 1% of the time
where the time goes in v11:
time: 32.3 us; the launch traced here: 32.2 us
  Pallas kernels  30.3 us (94%)
  between operations  0.67 us (2%)
  local copies, waits for them, and re-layouts  0.65 us (2%)
  other arithmetic  0.59 us (2%)
    pallas_call x1, Pallas kernels, device_image(): pl.pallas_call(image_kernel, out_shape=jax.ShapeDtypeStruct((2, TAYLOR, L...  30.3 us
    unnamed x2, local copies, waits for them, and re-layouts  0.65 us

profile of v11, /device:TPU:1, one launch (start us, length us, event | category | flops | bytes accessed | tf_op | source)
XLA Modules:
  0.0 32.2 jit_solution(10362138044479425123)
XLA Ops:
  0.7 0.0 copy-start
  0.7 0.6 %copy-done = f32[1,16]{1,0:T(1,128)S(1)} copy-done((f32[1,16]{1,0:T(1,128)S(1)}, f32[1,16]{1,0:T(1,128)}, u32[]{:S(2)}) %copy-start) | copy-done | bytes 88
  1.3 30.3 %strip_image.1 = f32[2,3,128]{2,1,0:T(4,128)S(1)} custom-call(f32[1,16]{1,0:T(1,128)S(1)} %copy-done, s32[1,1]{1,0:T(1,128)S(6)} %copy.13.refs_1_, bf16[2,2048]{1,0:T(2,128)(2,1)} %bitcast.9, bf16[1,2048]{1,0:T(2,128)(2,1)} %bitcast.10, bf16[64,2048]{1,0:T(8,128)(2,1)} %bitcast.8, s32[1,2048]{1,0:T(1,128)} %bitcast.11, s32[1,2048]{1,0:T(1,128)} %bitcast.12, ...), custom_call_target="tpu_custom_call" | custom-call | tf_op jit(solution)/shard_map/strip_image/pallas_call | solution.py:397
  31.6 0.6 %fusion = f32[3,128]{1,0:T(4,128)} fusion(f32[2,3,128]{2,1,0:T(4,128)S(1)} %strip_image.1), kind=kLoop, calls=%fused_computation.1 | loop fusion | flops 384 | bytes 4608 | tf_op jit(solution)/shard_map/div | solution.py:449
Async XLA Ops:
  0.7 0.7 %copy-start = (f32[1,16]{1,0:T(1,128)S(1)}, f32[1,16]{1,0:T(1,128)}, u32[]{:S(2)}) copy-start(f32[1,16]{1,0:T(1,128)} %refs_0_.1) | copy-start | bytes 196
